TPU v7x, 32 devices: a 4x2x2 block of a 4x4x8 slice. The times are simulated.
32 devices in a mesh: dp: 4 (over y, z), sp: 8 (over x, core).
Axes of the slice: x: 4, y: 2, z: 2, core: 2. Of those that a mesh axis runs over, the one named last changes fastest.
The devices are a block of a 4x4x8 slice.
Arguments:
- x_in: bfloat16 [8192, 2560], P(('dp', 'sp')), parts along dimension 0
- seg_id: int32 [8192], P(('dp', 'sp')), parts along dimension 0
- pos_id: int32 [8192], P(('dp', 'sp')), parts along dimension 0
- w_dq: bfloat16 [2560, 768], replicated
- g_q: bfloat16 [768], replicated
- w_uq: bfloat16 [768, 24576], replicated
- w_dkv: bfloat16 [2560, 576], replicated
- g_kv: bfloat16 [512], replicated
- w_ukv: bfloat16 [512, 32768], replicated
- w_o: bfloat16 [16384, 2560], replicated
- g_ffn: bfloat16 [2560], replicated
- w_gate: bfloat16 [2560, 6144], P(None, 'sp')
- w_up: bfloat16 [2560, 6144], P(None, 'sp')
- w_down: bfloat16 [6144, 2560], P('sp')
Outputs:
- output: bfloat16 [8192, 2560], P(('dp', 'sp')), parts along dimension 0
There are 4 independent parts. A program takes and returns all parts, laid end to end along the dimension named above; an argument that names none is the same for every part.
All inputs are finite; a program needn't handle non-finite values.
Results may differ from a plain program's by a relative error of at most 0.0150041.
Values are sent between devices in bfloat16 or wider.
A program may use at most 768 MiB of HBM per device.

v0:
```python
import functools
import jax
import jax.numpy as jnp
from jax import lax
from jax.experimental import pallas as pl
from jax.experimental.pallas import tpu as pltpu
from jax.sharding import PartitionSpec as P

NOPE_DIM = 128
ROPE_DIM = 64
VALUE_DIM = 128
KV_LATENT = 512
QK_DIM = NOPE_DIM + ROPE_DIM
KV_DIM = NOPE_DIM + VALUE_DIM
SCORE_SCALE = QK_DIM ** -0.5
LOG2E = 1.4426950408889634
NEG = -2.0e38
F32 = jnp.float32
BF16 = jnp.bfloat16


def rms_norm(vec_in, gain_vec):
    mean_sq = jnp.mean(vec_in * vec_in, axis=-1, keepdims=True)
    return vec_in * lax.rsqrt(mean_sq + 1e-6) * gain_vec.astype(F32)


def rope_tables(positions):
    half_dim = ROPE_DIM // 2
    inv_freq = 10000.0 ** (-jnp.arange(half_dim, dtype=F32) / half_dim)
    angles = positions.astype(F32)[..., None] * inv_freq
    return jnp.cos(angles), jnp.sin(angles)


def attn_body(core_ref, lo_ref, mid_ref, blk_ref, ckv_ref, kr_ref, cqa_ref, cqb_ref, cos_ref, sin_ref, start_ref,
              wuq_ref, wukv_ref, o_ref, kcat, vt, qcat, acc):
    i = pl.program_id(0)
    tok = ckv_ref.shape[0]
    qb = cqa_ref.shape[0]
    kb = qb

    @pl.when(i == 0)
    def _():
        kr = kr_ref[...]
        pad = jnp.concatenate([kr, jnp.zeros_like(kr)], axis=1)
        for h in range(2):
            kcat[h, :, NOPE_DIM:] = pad

    for r in range(tok // 512):
        rows = pl.ds(r * 512, 512)
        e = jnp.dot(ckv_ref[rows, :], wukv_ref[...], preferred_element_type=F32).astype(BF16)
        for h in range(2):
            kcat[h, rows, :NOPE_DIM] = e[:, KV_DIM * h:KV_DIM * h + NOPE_DIM]
            vt[h, :, rows] = e[:, KV_DIM * h + NOPE_DIM:KV_DIM * (h + 1)].T

    for b, cq in enumerate((cqa_ref, cqb_ref)):
        rows = pl.ds(b * qb, qb)
        q = jnp.dot(cq[...], wuq_ref[...], preferred_element_type=F32)
        q_r = jnp.concatenate([q[:, NOPE_DIM:QK_DIM], q[:, QK_DIM + NOPE_DIM:]], axis=1)
        lane = lax.broadcasted_iota(jnp.int32, q_r.shape, 1)
        lo_half = (lane % ROPE_DIM) < (ROPE_DIM // 2)
        swapped = jnp.where(lo_half, pltpu.roll(q_r, 2 * ROPE_DIM - ROPE_DIM // 2, 1), pltpu.roll(q_r, ROPE_DIM // 2, 1))
        q_r = (q_r * cos_ref[rows, :] + swapped * sin_ref[rows, :]).astype(BF16)
        zero = jnp.zeros((qb, ROPE_DIM), BF16)
        for h in range(2):
            qcat[h, rows, :NOPE_DIM] = q[:, QK_DIM * h:QK_DIM * h + NOPE_DIM].astype(BF16)
            qcat[h, rows, NOPE_DIM:] = jnp.concatenate([q_r[:, ROPE_DIM * h:ROPE_DIM * (h + 1)], zero], axis=1)

    for b in range(2):
        qrows = pl.ds(b * qb, qb)
        t0 = blk_ref[b] * qb

        def step(j, carry, masked):
            k0 = pl.multiple_of(j * kb, kb)
            krows = pl.ds(k0, kb)
            new = []
            for h in range(2):
                m, l = carry[2 * h], carry[2 * h + 1]
                s = lax.dot_general(kcat[h, krows, :], qcat[h, qrows, :], (((1,), (1,)), ((), ())),
                                    preferred_element_type=F32)
                s = s * (SCORE_SCALE * LOG2E)
                if masked:
                    r = k0 + lax.broadcasted_iota(jnp.int32, s.shape, 0)
                    t = t0 + lax.broadcasted_iota(jnp.int32, s.shape, 1)
                    s = jnp.where((r <= t) & (r >= start_ref[:, qrows]), s, NEG)
                m_new = jnp.maximum(m, jnp.max(s, axis=0, keepdims=True))
                alpha = jnp.exp2(m - m_new)
                p = jnp.exp2(s - m_new)
                l = alpha * l + jnp.sum(p, axis=0, keepdims=True)
                acc[h] = acc[h] * alpha + jnp.dot(vt[h, :, krows], p.astype(BF16), preferred_element_type=F32)
                new += [m_new, l]
            return tuple(new)

        acc[...] = jnp.zeros_like(acc)
        init = (jnp.full((1, qb), NEG, F32), jnp.zeros((1, qb), F32)) * 2
        carry = lax.fori_loop(lo_ref[b], mid_ref[b], functools.partial(step, masked=True), init)
        carry = lax.fori_loop(mid_ref[b], blk_ref[b], functools.partial(step, masked=False), carry)
        carry = step(blk_ref[b], carry, True)
        for h in range(2):
            o = (acc[h] * (1.0 / carry[2 * h + 1])).astype(BF16)
            o_ref[qrows, VALUE_DIM * h:VALUE_DIM * (h + 1)] = o.T


def attention(core, lo, mid, blk, ckv, kr, cqa, cqb, cos, sin, start, w_uq, w_ukv):
    tok = ckv.shape[0]
    qb, q_lat = cqa.shape
    heads = w_uq.shape[1] // QK_DIM
    pairs = heads // 4
    full = lambda shape: pl.BlockSpec(shape, lambda i, *_: (0, 0))
    return pl.pallas_call(
        attn_body,
        grid_spec=pltpu.PrefetchScalarGridSpec(
            num_scalar_prefetch=4,
            grid=(pairs,),
            in_specs=[
                full(ckv.shape), full(kr.shape), full(cqa.shape), full(cqb.shape), full(cos.shape), full(sin.shape),
                full(start.shape),
                pl.BlockSpec((q_lat, 2 * QK_DIM), lambda i, core, *_: (0, core[0] * pairs + i)),
                pl.BlockSpec((KV_LATENT, 2 * KV_DIM), lambda i, core, *_: (0, core[0] * pairs + i)),
            ],
            out_specs=pl.BlockSpec((2 * qb, 2 * VALUE_DIM), lambda i, *_: (0, i)),
            scratch_shapes=[
                pltpu.VMEM((2, tok, 2 * NOPE_DIM), BF16),
                pltpu.VMEM((2, VALUE_DIM, tok), BF16),
                pltpu.VMEM((2, 2 * qb, 2 * NOPE_DIM), BF16),
                pltpu.VMEM((2, VALUE_DIM, qb), F32),
            ]),
        out_shape=jax.ShapeDtypeStruct((2 * qb, heads // 2 * VALUE_DIM), BF16),
        compiler_params=pltpu.CompilerParams(dimension_semantics=("arbitrary",), vmem_limit_bytes=60 * 2 ** 20),
        cost_estimate=pl.CostEstimate(flops=80 * 10 ** 9, bytes_accessed=45 * 10 ** 6, transcendentals=40 * 10 ** 6),
    )(core, lo, mid, blk, ckv, kr, cqa, cqb, cos, sin, start, w_uq, w_ukv)


def tail_body(chips, o_hbm, wo_hbm, wg_hbm, wg2_hbm, wu_hbm, wu2_hbm, wd_hbm, wd2_hbm, g_ref, out_ref,
              obuf, wbuf, acc, xr, yall, hbuf, wg, wu, act, rsr, rss,
              o_sem, w_sem, f_sem, d_sem, xs_sem, xr_sem, as_sem, ar_sem, fs_sem, fr_sem, ss_sem, sr_sem):
    me = lax.axis_index('sp')
    chip, core = me // 2, me % 2
    right, left = (chip + 1) % chips, (chip + chips - 1) % chips
    far = (chip + 2) % chips
    ring = (2 * right + core, 2 * left + core)
    peer = 2 * chip + 1 - core
    src = (left, right)
    nt, kt = acc.shape[0], obuf.shape[1] // wbuf.shape[1]
    nbuf, tk, tn = wbuf.shape
    blk = yall.shape[2]
    half = blk // 2
    depth = kt * tk
    shard = wg_hbm.shape[1]

    def slot_of(q):
        return core * (chips - 1) + (1 - 2 * core) * q

    def remote(s, d, ssem, rsem, dev):
        return pltpu.make_async_remote_copy(src_ref=s, dst_ref=d, send_sem=ssem, recv_sem=rsem,
                                            device_id={'sp': dev}, device_id_type=pl.DeviceIdType.MESH)

    def w_copy(t):
        n, k = t // kt, t % kt
        return pltpu.make_async_copy(
            wo_hbm.at[pl.ds(pl.multiple_of(core * depth + k * tk, tk), tk), pl.ds(pl.multiple_of(n * tn, tn), tn)],
            wbuf.at[t % nbuf], w_sem.at[t % nbuf])

    def o_copy(k):
        cols = pl.ds(pl.multiple_of(k * tk, tk), tk)
        return pltpu.make_async_copy(o_hbm.at[:, cols], obuf.at[:, cols], o_sem.at[k])

    f_copies = [pltpu.make_async_copy(s, d.at[:, pl.ds(c * shard, shard)], f_sem.at[i])
                for i, (s, d, c) in enumerate(((wg_hbm, wg, 0), (wg2_hbm, wg, 1), (wu_hbm, wu, 0), (wu2_hbm, wu, 1)))]
    grain = 256
    width = nt * tn
    n_grain = 2 * shard // grain
    per = obuf.shape[0] // grain
    d_copies = []
    for g in range(n_grain):
        s = wd_hbm if g < n_grain // 2 else wd2_hbm
        d_copies.append(pltpu.make_async_copy(
            s.at[pl.ds((g % (n_grain // 2)) * grain, grain), :],
            obuf.at[pl.ds((g % per) * grain, grain), pl.ds((g // per) * width, width)], d_sem.at[g]))

    for k in range(kt):
        o_copy(k).start()
    for t in range(nbuf - 1):
        w_copy(t).start()

    barrier = pltpu.get_barrier_semaphore()
    for dev in (peer,) + ring:
        pl.semaphore_signal(barrier, inc=1, device_id={'sp': dev}, device_id_type=pl.DeviceIdType.MESH)
    pl.semaphore_wait(barrier, 3)

    own_rows = pl.ds(pl.multiple_of(core * blk, blk), blk)
    peer_rows = pl.ds(pl.multiple_of((1 - core) * blk, blk), blk)

    def x_copy(n):
        return remote(acc.at[n, peer_rows, :], xr.at[n], xs_sem.at[n], xr_sem.at[n], peer)

    def a_copy(d, n, slot):
        return remote(yall.at[slot, n], yall.at[slot, n], as_sem.at[d, n], ar_sem.at[d, n], ring[d])

    def f_copy(d, n, slot):
        rows = pl.ds(d * half, half)
        return remote(yall.at[slot, n, rows, :], yall.at[slot, n, rows, :], fs_sem.at[d, n], fr_sem.at[d, n], ring[d])

    def combine(n):
        x_copy(n).wait_recv()
        yall[chip, n] = (acc[n, own_rows, :] + xr[n]).astype(BF16)
        for d in range(2):
            a_copy(d, n, chip).start()

    def forward(n):
        for d in range(2):
            a_copy(d, n, src[d]).wait_recv()
            f_copy(d, n, src[d]).start()

    def w_step(t, _):
        n, k = t // kt, t % kt

        @pl.when(t + nbuf - 1 < nt * kt)
        def _():
            w_copy(t + nbuf - 1).start()

        @pl.when(t == nbuf)
        def _():
            for c in f_copies:
                c.start()

        @pl.when(n == 0)
        def _():
            o_copy(k).wait()
        w_copy(t).wait()
        prod = jnp.dot(obuf[:, pl.ds(pl.multiple_of(k * tk, tk), tk)], wbuf[t % nbuf], preferred_element_type=F32)

        @pl.when(k == 0)
        def _():
            acc[n] = prod

        @pl.when(k > 0)
        def _():
            acc[n] += prod

        @pl.when(k == kt - 1)
        def _():
            x_copy(n).start()

            @pl.when(n >= 1)
            def _():
                combine(n - 1)

            @pl.when(n >= 3)
            def _():
                forward(n - 3)
        return 0

    lax.fori_loop(0, nt * kt, w_step, 0)
    for c in d_copies:
        c.start()
    combine(nt - 1)
    forward(nt - 3)

    def activate(slot):
        def norm(r, _):
            rows = pl.ds(pl.multiple_of(r * 64, 64), 64)
            ys = [yall[slot, k, rows, :].astype(F32) for k in range(nt)]
            total = sum(jnp.sum(y * y, axis=-1, keepdims=True) for y in ys)
            scale = lax.rsqrt(total * (1.0 / width) + 1e-6)
            for k in range(nt):
                gain = g_ref[:, pl.ds(k * tn, tn)].astype(F32)
                hbuf[k, rows, :] = (ys[k] * scale * gain).astype(BF16)
            return 0
        lax.fori_loop(0, blk // 64, norm, 0)

        def cols(c, _):
            cs = pl.ds(pl.multiple_of(c * 256, 256), 256)
            gate = sum(jnp.dot(hbuf[k], wg[pl.ds(k * tn, tn), cs], preferred_element_type=F32) for k in range(nt))
            up = sum(jnp.dot(hbuf[k], wu[pl.ds(k * tn, tn), cs], preferred_element_type=F32) for k in range(nt))
            act[slot, :, cs] = (jax.nn.silu(gate) * up).astype(BF16)
            return 0
        lax.fori_loop(0, 2 * shard // 256, cols, 0)

    hw = width // 2

    def down(slot, c, d):
        rows = pl.ds(c * half, half)
        return sum(jnp.dot(act[slot, rows, pl.ds(g * grain, grain)],
                           obuf[pl.ds((g % per) * grain, grain), pl.ds((g // per) * width + d * hw, hw)],
                           preferred_element_type=F32) for g in range(n_grain))

    def s_copy(d, s, c):
        src_ref = rss.at[d, c] if s == 0 else rsr.at[d, s - 1, c]
        return remote(src_ref, rsr.at[d, s, c], ss_sem.at[d, s, c], sr_sem.at[d, s, c], ring[d])

    def first():
        for d, q in enumerate((left, right)):
            for c in range(2):
                rss[d, c] = down(slot_of(q), c, d)
                s_copy(d, 0, c).start()

    for c in f_copies:
        c.wait()
    activate(chip)
    forward(nt - 2)
    forward(nt - 1)
    for c in d_copies:
        c.wait()
    activate(left)
    activate(right)

    @pl.when(core == 0)
    def _():
        first()
    for n in range(nt):
        for d in range(2):
            f_copy(d, n, far).wait_recv()
    activate(far)

    @pl.when(core == 1)
    def _():
        first()

    for s, dests in ((1, (far, far)), (2, (right, left))):
        for c in range(2):
            for d in range(2):
                part = down(slot_of(dests[d]), c, d)
                s_copy(d, s - 1, c).wait_recv()
                rsr[d, s - 1, c] = rsr[d, s - 1, c] + part
                s_copy(d, s, c).start()

    mine = slot_of(chip)
    per_half = hw // half
    for c in range(2):
        rows = pl.ds(c * half, half)
        for d in range(2):
            part = down(mine, c, d)
            s_copy(d, 2, c).wait_recv()
            pieces = []
            for col in range(d * hw, (d + 1) * hw, 256):
                pieces.append(yall[mine, col // tn, rows, pl.ds(col % tn, 256)].astype(F32))
            y = jnp.concatenate(pieces, axis=1)
            out_ref[rows, pl.ds(d * hw, hw)] = (y + (rsr[d, 2, c] + part)).astype(BF16)

    for n in range(nt):
        x_copy(n).wait_send()
        for d in range(2):
            a_copy(d, n, chip).wait_send()
            f_copy(d, n, src[d]).wait_send()
    for d in range(2):
        for s in range(3):
            for c in range(2):
                s_copy(d, s, c).wait_send()


def tail(chips, o, w_o, w_gate, w_gate2, w_up, w_up2, w_down, w_down2, g_ffn, nbuf=4, tk=1024, tn=512):
    rows, depth = o.shape
    width = w_o.shape[1]
    shard = w_gate.shape[1]
    blk = rows // 2
    nt, kt = width // tn, depth // tk
    dma = pltpu.SemaphoreType.DMA
    hbm = pl.BlockSpec(memory_space=pl.ANY)
    vmem = pl.BlockSpec(memory_space=pltpu.VMEM)
    return pl.pallas_call(
        functools.partial(tail_body, chips),
        in_specs=[hbm] * 8 + [vmem],
        out_specs=vmem,
        out_shape=jax.ShapeDtypeStruct((blk, width), BF16),
        scratch_shapes=[
            pltpu.VMEM((rows, depth), BF16),
            pltpu.VMEM((nbuf, tk, tn), BF16),
            pltpu.VMEM((nt, rows, tn), F32),
            pltpu.VMEM((nt, blk, tn), F32),
            pltpu.VMEM((chips, nt, blk, tn), BF16),
            pltpu.VMEM((nt, blk, tn), BF16),
            pltpu.VMEM((width, 2 * shard), BF16),
            pltpu.VMEM((width, 2 * shard), BF16),
            pltpu.VMEM((chips, blk, 2 * shard), BF16),
            pltpu.VMEM((2, 3, 2, blk // 2, width // 2), F32),
            pltpu.VMEM((2, 2, blk // 2, width // 2), F32),
            dma((kt,)), dma((nbuf,)), dma((4,)), dma((2 * shard // 256,)),
            dma((nt,)), dma((nt,)), dma((2, nt)), dma((2, nt)), dma((2, nt)), dma((2, nt)),
            dma((2, 3, 2)), dma((2, 3, 2)),
        ],
        compiler_params=pltpu.CompilerParams(collective_id=0, has_side_effects=True,
                                             vmem_limit_bytes=63 * 2 ** 20),
        cost_estimate=pl.CostEstimate(flops=46 * 10 ** 9, bytes_accessed=75 * 10 ** 6, transcendentals=10 ** 6),
    )(o, w_o, w_gate, w_gate2, w_up, w_up2, w_down, w_down2, g_ffn)


def solution(mesh):
    group_size = mesh.shape['sp']
    chips = group_size // 2
    tok_spec = P(('dp', 'sp'), None)
    row_spec = P(('dp', 'sp'))
    full_spec = P()
    col_spec = P(None, 'sp')
    swap = [(d, d ^ 1) for d in range(group_size)]

    def device_fn(x_blk, seg_blk, pos_blk, w_dq, g_q, w_uq, w_dkv, g_kv, w_ukv, w_o, g_ffn, w_gate, w_up, w_down):
        me = lax.axis_index('sp')
        chip, core = me // 2, me % 2
        blk_len = x_blk.shape[0]
        core_arr = core.reshape(1).astype(jnp.int32)

        w_gate2 = lax.ppermute(w_gate, 'sp', swap)
        w_up2 = lax.ppermute(w_up, 'sp', swap)
        w_down2 = lax.ppermute(w_down, 'sp', swap)

        q_lin = jnp.dot(x_blk, w_dq, preferred_element_type=F32)
        c_q = rms_norm(q_lin, g_q).astype(BF16)
        kv_lin = jnp.dot(x_blk, w_dkv, preferred_element_type=F32)
        c_kv = rms_norm(kv_lin[:, :KV_LATENT], g_kv).astype(BF16)
        cosine, sine = rope_tables(pos_blk)
        lo_half, hi_half = kv_lin[:, KV_LATENT:KV_LATENT + ROPE_DIM // 2], kv_lin[:, KV_LATENT + ROPE_DIM // 2:]
        k_rope = jnp.concatenate([lo_half * cosine - hi_half * sine, hi_half * cosine + lo_half * sine],
                                 axis=-1).astype(BF16)
        gather = lambda a: lax.all_gather(a, 'sp', axis=0, tiled=True)
        cq_all, ckv_all, kr_all, pos_all = gather(c_q), gather(c_kv), gather(k_rope), gather(pos_blk)

        blk = jnp.stack([2 * chip, group_size - 1 - 2 * chip]).astype(jnp.int32)
        take = lambda a, b: lax.dynamic_slice_in_dim(a, blk[b] * blk_len, blk_len, axis=0)
        cqa, cqb = take(cq_all, 0), take(cq_all, 1)
        pos_q = jnp.concatenate([take(pos_all, 0), take(pos_all, 1)])
        rows_q = (blk[:, None] * blk_len + jnp.arange(blk_len, dtype=jnp.int32)[None, :]).reshape(-1)
        start = rows_q - pos_q
        cosine, sine = rope_tables(pos_q)
        cos4 = jnp.concatenate([cosine] * 4, axis=1)
        sin4 = jnp.concatenate([-sine, sine, -sine, sine], axis=1)
        lo = start.reshape(2, blk_len)[:, 0] // blk_len
        last = start.reshape(2, blk_len)[:, -1]
        mid = jnp.minimum((last + blk_len - 1) // blk_len, blk)
        mid = jnp.maximum(mid, lo)

        o = attention(core_arr, lo, mid, blk, ckv_all, kr_all, cqa, cqb, cos4, sin4, start[None, :], w_uq, w_ukv)
        return tail(chips, o, w_o, w_gate, w_gate2, w_up, w_up2, w_down, w_down2, g_ffn[None, :])

    return jax.shard_map(device_fn, mesh=mesh, in_specs=(tok_spec, row_spec, row_spec, full_spec, full_spec, full_spec, full_spec, full_spec, full_spec, full_spec, full_spec, col_spec, col_spec, P('sp', None)), out_specs=tok_spec, check_vma=False)
```

profile of v0, /device:TPU:121, one launch (start us, length us, event | category | flops | bytes accessed | tf_op | source)
XLA Modules:
  0.0 533.8 jit_solution(15997825176269484791)
XLA Ops:
  6.6 3.9 multiply_reduce_fusion
  10.5 0.9 multiply_convert_fusion
  11.5 3.1 fusion.14
  14.6 0.1 multiply_reduce_fusion.1
  14.7 0.8 multiply_convert_fusion.1
  15.6 0.7 collective-permute-start
  16.3 0.1 collective-permute-start.1
  16.4 0.4 collective-permute-start.2
  16.8 25.1 %all-gather = s32[8,1,256]{2,1,0:T(1,128)S(1)} all-gather(s32[1,1,256]{2,1,0:T(1,128)S(1)} %bitcast.19), channel_id=1, replica_groups=mesh['dp'=4,'sp'=8] {'sp'}, dimensions={0}, use_global_device_ids=true | all-gather | bytes 9216 | tf_op jit(solution)/shard_map/all_gather | solution.py:414
  42.0 0.1 fusion.13
  42.1 0.1 broadcast_multiply_fusion
  42.2 0.6 broadcast_in_dim.2.g_ref
  42.9 0.2 fusion.11
  43.0 0.6 fusion.5
  43.6 0.1 pad_maximum_fusion.2
  43.7 13.9 %all_gather.14.kr_ref = bf16[2048,64]{1,0:T(8,128)(2,1)} all-gather(bf16[256,64]{1,0:T(8,128)(2,1)S(1)} %pad_maximum_fusion.2), channel_id=1, replica_groups=mesh['dp'=4,'sp'=8] {'sp'}, dimensions={0}, use_global_device_ids=true | all-gather | bytes 294912 | tf_op jit(solution)/shard_map/all_gather | solution.py:414
  57.6 1.0 fusion.8
  58.6 1.3 pad_maximum_fusion
  59.9 0.6 minimum_maximum_fusion
  60.5 0.6 add_subtract_fusion.start_ref
  61.1 2.1 constant_dynamic-slice_fusion
  63.1 298.5 %shard_map.127.o_hbm = bf16[512,8192]{1,0:T(8,128)(2,1)} custom-call(s32[1]{0:T(128)} %bitcast.core_ref, s32[2]{0:T(128)} %get-tuple-element.8.lo_ref, s32[2]{0:T(128)} %get-tuple-element.7.mid_ref, s32[2]{0:T(128)} %copy-done.3, bf16[2048,512]{1,0:T(8,128)(2,1)} %all-gather.4.cloned.1.call-done.ckv_ref, bf16[2048,64]{1,0:T(8,128)(2,1)} %all_gather.14.kr_ref, ...), custom_call_target="tpu_custom_call" | custom-call | flops 80000000000 | bytes 45000000 | tf_op jit(solution)/shard_map/pallas_call | solution.py:109
  361.6 162.9 %shard_map.128 = bf16[256,2560]{1,0:T(8,128)(2,1)} custom-call(bf16[512,8192]{1,0:T(8,128)(2,1)} %shard_map.127.o_hbm, bf16[16384,2560]{1,0:T(8,128)(2,1)} %wo_hbm.1, bf16[2560,768]{1,0:T(8,128)(2,1)} %wg_hbm.1, bf16[2560,768]{1,0:T(8,128)(2,1)} %collective-permute-done.wg2_hbm, bf16[2560,768]{1,0:T(8,128)(2,1)} %wu_hbm.1, ...), custom_call_target="tpu_custom_call" | custom-call | flops 46000001024 | bytes 75000000 | tf_op jit(solution)/shard_map/pallas_call | solution.py:360
  524.5 2.5 copy.35
  (31 shorter events, 0.4 us)
Async XLA Ops:
  6.5 5.0 copy-start.5
  6.5 3.9 copy-start.2
  6.6 4.9 copy-start.4
  6.6 54.5 %all-gather.6.cloned.1.call-start = ((), (), s32[]{:S(2)}) async-start(), calls=%async_computation.1 | async-start | bytes 3538944 | tf_op jit(solution)/shard_map/all_gather | solution.py:414
  11.4 51.7 %all-gather.4.cloned.1.call-start = ((), (), s32[]{:S(2)}) async-start(), calls=%async_computation | async-start | bytes 2359296 | tf_op jit(solution)/shard_map/all_gather | solution.py:414
  11.5 5.3 copy-start.1
  11.5 30.7 %copy-start = (bf16[2560]{0:T(1024)(128)(2,1)S(1)}, bf16[2560]{0:T(1024)(128)(2,1)}, u32[]{:S(2)}) copy-start(bf16[2560]{0:T(1024)(128)(2,1)} %param.23) | copy-start | bytes 15364
  15.6 346.0 %collective-permute-start = (bf16[2560,768]{1,0:T(8,128)(2,1)}, bf16[2560,768]{1,0:T(8,128)(2,1)}, u32[]{:S(2)}, u32[]{:S(2)}) collective-permute-start(bf16[2560,768]{1,0:T(8,128)(2,1)} %wg_hbm.1), channel_id=1, source_target_pairs={{0,1},{1,0},{2,3},{3,2},{4,5},{5,4},{6,7},{7,6},{8,9},{9,8},{10,11... | collective-permute-start | bytes 11796488 | tf_op jit(solution)/shard_map/ppermute | solution.py:402
  16.3 345.3 %collective-permute-start.1 = (bf16[2560,768]{1,0:T(8,128)(2,1)}, bf16[2560,768]{1,0:T(8,128)(2,1)}, u32[]{:S(2)}, u32[]{:S(2)}) collective-permute-start(bf16[2560,768]{1,0:T(8,128)(2,1)} %wu_hbm.1), channel_id=1, source_target_pairs={{0,1},{1,0},{2,3},{3,2},{4,5},{5,4},{6,7},{7,6},{8,9},{9,8},{10,11... | collective-permute-start | bytes 11796488 | tf_op jit(solution)/shard_map/ppermute | solution.py:403
  16.4 345.1 %collective-permute-start.2 = (bf16[768,2560]{1,0:T(8,128)(2,1)}, bf16[768,2560]{1,0:T(8,128)(2,1)}, u32[]{:S(2)}, u32[]{:S(2)}) collective-permute-start(bf16[768,2560]{1,0:T(8,128)(2,1)} %wd_hbm.1), channel_id=1, source_target_pairs={{0,1},{1,0},{2,3},{3,2},{4,5},{5,4},{6,7},{7,6},{8,9},{9,8},{10,11... | collective-permute-start | bytes 11796488 | tf_op jit(solution)/shard_map/ppermute | solution.py:404
  42.2 21.0 %copy-start.3 = (s32[2]{0:T(128)}, s32[2]{0:T(128)S(1)}, u32[]{:S(2)}) copy-start(s32[2]{0:T(128)S(1)} %get-tuple-element.10.blk_ref) | copy-start | bytes 28
Sparse Core Ops, SparseCore 0:
  11.5 26.2 all-gather.5
  39.4 22.9 all-gather.3
where the time goes:
time: 534 us
  Pallas kernels  461 us (86%)
  blocking collectives  39.1 us (7%)
  between operations  13.6 us (3%)
  matrix products  6.92 us (1%)
  other arithmetic  6.28 us (1%)
    pallas_call x1, Pallas kernels, attention(): pl.pallas_call(attn_body, grid_spec=pltpu.PrefetchScalarGridSpec(num_scal...  298 us
    pallas_call x1, Pallas kernels, tail(): pl.pallas_call(functools.partial(tail_body, chips), in_specs=[hbm] * 8 +...  163 us
    all_gather x2, blocking collectives, device_fn(): gather = lambda a: lax.all_gather(a, 'sp', axis=0, tiled=True)  39.1 us
  transfers between devices with their start and end apart: 5, of which 0 were waited for; matrix products, arithmetic and copies ran while one was open for 2% of the time, Pallas kernels for 56%

commit v1 on v0

--- a/solution.py
+++ b/solution.py
@@ -32,11 +32,11 @@
 
 
 def attn_body(core_ref, lo_ref, mid_ref, blk_ref, ckv_ref, kr_ref, cqa_ref, cqb_ref, cos_ref, sin_ref, start_ref,
-              wuq_ref, wukv_ref, o_ref, kcat, vt, qcat, acc):
+              wuq_ref, wukv_ref, o_ref, kcat, vt, qcat, sbuf, mbuf, acc, *, kb):
     i = pl.program_id(0)
     tok = ckv_ref.shape[0]
     qb = cqa_ref.shape[0]
-    kb = qb
+    cur, prev = i % 2, (i + 1) % 2
 
     @pl.when(i == 0)
     def _():
@@ -50,7 +50,7 @@
         e = jnp.dot(ckv_ref[rows, :], wukv_ref[...], preferred_element_type=F32).astype(BF16)
         for h in range(2):
             kcat[h, rows, :NOPE_DIM] = e[:, KV_DIM * h:KV_DIM * h + NOPE_DIM]
-            vt[h, :, rows] = e[:, KV_DIM * h + NOPE_DIM:KV_DIM * (h + 1)].T
+            vt[cur, h, :, rows] = e[:, KV_DIM * h + NOPE_DIM:KV_DIM * (h + 1)].T
 
     for b, cq in enumerate((cqa_ref, cqb_ref)):
         rows = pl.ds(b * qb, qb)
@@ -62,11 +62,10 @@
         q_r = (q_r * cos_ref[rows, :] + swapped * sin_ref[rows, :]).astype(BF16)
         zero = jnp.zeros((qb, ROPE_DIM), BF16)
         for h in range(2):
-            qcat[h, rows, :NOPE_DIM] = q[:, QK_DIM * h:QK_DIM * h + NOPE_DIM].astype(BF16)
-            qcat[h, rows, NOPE_DIM:] = jnp.concatenate([q_r[:, ROPE_DIM * h:ROPE_DIM * (h + 1)], zero], axis=1)
-
-    for b in range(2):
-        qrows = pl.ds(b * qb, qb)
+            qcat[b, h, :, :NOPE_DIM] = q[:, QK_DIM * h:QK_DIM * h + NOPE_DIM].astype(BF16)
+            qcat[b, h, :, NOPE_DIM:] = jnp.concatenate([q_r[:, ROPE_DIM * h:ROPE_DIM * (h + 1)], zero], axis=1)
+
+    def q_block(b, _):
         t0 = blk_ref[b] * qb
 
         def step(j, carry, masked):
@@ -75,57 +74,66 @@
             new = []
             for h in range(2):
                 m, l = carry[2 * h], carry[2 * h + 1]
-                s = lax.dot_general(kcat[h, krows, :], qcat[h, qrows, :], (((1,), (1,)), ((), ())),
+                s = lax.dot_general(kcat[h, krows, :], qcat[b, h], (((1,), (1,)), ((), ())),
                                     preferred_element_type=F32)
                 s = s * (SCORE_SCALE * LOG2E)
                 if masked:
                     r = k0 + lax.broadcasted_iota(jnp.int32, s.shape, 0)
                     t = t0 + lax.broadcasted_iota(jnp.int32, s.shape, 1)
-                    s = jnp.where((r <= t) & (r >= start_ref[:, qrows]), s, NEG)
-                m_new = jnp.maximum(m, jnp.max(s, axis=0, keepdims=True))
-                alpha = jnp.exp2(m - m_new)
-                p = jnp.exp2(s - m_new)
-                l = alpha * l + jnp.sum(p, axis=0, keepdims=True)
-                acc[h] = acc[h] * alpha + jnp.dot(vt[h, :, krows], p.astype(BF16), preferred_element_type=F32)
-                new += [m_new, l]
+                    s = jnp.where((r <= t) & (r >= start_ref[b]), s, NEG)
+                m = jnp.maximum(m, jnp.max(s.reshape(kb // 8, 8, qb), axis=0))
+                p = jnp.exp2(sbuf[prev, b, h, krows, :] - mbuf[prev, b, h])
+                l = l + jnp.sum(p.reshape(kb // 8, 8, qb), axis=0)
+                acc[h] += jnp.dot(vt[prev, h, :, krows], p.astype(BF16), preferred_element_type=F32)
+                sbuf[cur, b, h, krows, :] = s
+                new += [m, l]
             return tuple(new)
 
         acc[...] = jnp.zeros_like(acc)
-        init = (jnp.full((1, qb), NEG, F32), jnp.zeros((1, qb), F32)) * 2
+        init = (jnp.full((8, qb), NEG, F32), jnp.zeros((8, qb), F32)) * 2
         carry = lax.fori_loop(lo_ref[b], mid_ref[b], functools.partial(step, masked=True), init)
-        carry = lax.fori_loop(mid_ref[b], blk_ref[b], functools.partial(step, masked=False), carry)
-        carry = step(blk_ref[b], carry, True)
+        last = (t0 + qb - 1) // kb
+        carry = lax.fori_loop(mid_ref[b], last, functools.partial(step, masked=False), carry)
+        carry = step(last, carry, True)
         for h in range(2):
-            o = (acc[h] * (1.0 / carry[2 * h + 1])).astype(BF16)
-            o_ref[qrows, VALUE_DIM * h:VALUE_DIM * (h + 1)] = o.T
-
-
-def attention(core, lo, mid, blk, ckv, kr, cqa, cqb, cos, sin, start, w_uq, w_ukv):
+            mbuf[cur, b, h] = jnp.max(carry[2 * h], axis=0, keepdims=True)
+            l = jnp.sum(carry[2 * h + 1], axis=0, keepdims=True)
+            o = (acc[h] * (1.0 / l)).astype(BF16)
+            o_ref[pl.ds(pl.multiple_of(b * qb, qb), qb), VALUE_DIM * h:VALUE_DIM * (h + 1)] = o.T
+        return 0
+
+    lax.fori_loop(0, 2, q_block, 0)
+
+
+def attention(core, lo, mid, blk, ckv, kr, cqa, cqb, cos, sin, start, w_uq, w_ukv, kb):
     tok = ckv.shape[0]
     qb, q_lat = cqa.shape
     heads = w_uq.shape[1] // QK_DIM
     pairs = heads // 4
-    full = lambda shape: pl.BlockSpec(shape, lambda i, *_: (0, 0))
+    full = lambda shape: pl.BlockSpec(shape, lambda i, *_: (0,) * len(shape), pipeline_mode=pl.Buffered(1))
+    group = lambda i, core: core[0] * pairs + jnp.minimum(i, pairs - 1)
     return pl.pallas_call(
-        attn_body,
+        functools.partial(attn_body, kb=kb),
         grid_spec=pltpu.PrefetchScalarGridSpec(
             num_scalar_prefetch=4,
-            grid=(pairs,),
+            grid=(pairs + 1,),
             in_specs=[
                 full(ckv.shape), full(kr.shape), full(cqa.shape), full(cqb.shape), full(cos.shape), full(sin.shape),
                 full(start.shape),
-                pl.BlockSpec((q_lat, 2 * QK_DIM), lambda i, core, *_: (0, core[0] * pairs + i)),
-                pl.BlockSpec((KV_LATENT, 2 * KV_DIM), lambda i, core, *_: (0, core[0] * pairs + i)),
+                pl.BlockSpec((q_lat, 2 * QK_DIM), lambda i, core, *_: (0, group(i, core))),
+                pl.BlockSpec((KV_LATENT, 2 * KV_DIM), lambda i, core, *_: (0, group(i, core))),
             ],
-            out_specs=pl.BlockSpec((2 * qb, 2 * VALUE_DIM), lambda i, *_: (0, i)),
+            out_specs=pl.BlockSpec((2 * qb, 2 * VALUE_DIM), lambda i, *_: (0, jnp.maximum(i - 1, 0))),
             scratch_shapes=[
                 pltpu.VMEM((2, tok, 2 * NOPE_DIM), BF16),
-                pltpu.VMEM((2, VALUE_DIM, tok), BF16),
-                pltpu.VMEM((2, 2 * qb, 2 * NOPE_DIM), BF16),
+                pltpu.VMEM((2, 2, VALUE_DIM, tok), BF16),
+                pltpu.VMEM((2, 2, qb, 2 * NOPE_DIM), BF16),
+                pltpu.VMEM((2, 2, 2, tok, qb), F32),
+                pltpu.VMEM((2, 2, 2, 1, qb), F32),
                 pltpu.VMEM((2, VALUE_DIM, qb), F32),
             ]),
         out_shape=jax.ShapeDtypeStruct((2 * qb, heads // 2 * VALUE_DIM), BF16),
-        compiler_params=pltpu.CompilerParams(dimension_semantics=("arbitrary",), vmem_limit_bytes=60 * 2 ** 20),
+        compiler_params=pltpu.CompilerParams(dimension_semantics=("arbitrary",), vmem_limit_bytes=62 * 2 ** 20),
         cost_estimate=pl.CostEstimate(flops=80 * 10 ** 9, bytes_accessed=45 * 10 ** 6, transcendentals=40 * 10 ** 6),
     )(core, lo, mid, blk, ckv, kr, cqa, cqb, cos, sin, start, w_uq, w_ukv)
 
@@ -423,12 +431,13 @@
         cosine, sine = rope_tables(pos_q)
         cos4 = jnp.concatenate([cosine] * 4, axis=1)
         sin4 = jnp.concatenate([-sine, sine, -sine, sine], axis=1)
-        lo = start.reshape(2, blk_len)[:, 0] // blk_len
-        last = start.reshape(2, blk_len)[:, -1]
-        mid = jnp.minimum((last + blk_len - 1) // blk_len, blk)
-        mid = jnp.maximum(mid, lo)
-
-        o = attention(core_arr, lo, mid, blk, ckv_all, kr_all, cqa, cqb, cos4, sin4, start[None, :], w_uq, w_ukv)
+        kb = 2 * blk_len
+        start = start.reshape(2, 1, blk_len)
+        lo = start[:, 0, 0] // kb
+        last = (blk * blk_len + blk_len - 1) // kb
+        mid = jnp.maximum(jnp.minimum((start[:, 0, -1] + kb - 1) // kb, last), lo)
+
+        o = attention(core_arr, lo, mid, blk, ckv_all, kr_all, cqa, cqb, cos4, sin4, start, w_uq, w_ukv, kb)
         return tail(chips, o, w_o, w_gate, w_gate2, w_up, w_up2, w_down, w_down2, g_ffn[None, :])
 
     return jax.shard_map(device_fn, mesh=mesh, in_specs=(tok_spec, row_spec, row_spec, full_spec, full_spec, full_spec, full_spec, full_spec, full_spec, full_spec, full_spec, col_spec, col_spec, P('sp', None)), out_specs=tok_spec, check_vma=False)

time: 534 us -> 404 us (0.76)
  the two profiles are of different devices: /device:TPU:121 before, /device:TPU:89 now
where the time goes in v1:
time: 404 us; the launch traced here: 402 us
  Pallas kernels  330 us (82%)
  blocking collectives  38.9 us (10%)
  between operations  13.6 us (3%)
  matrix products  6.93 us (2%)
  other arithmetic  5.71 us (1%)
  local copies, waits for them, and re-layouts  5.24 us (1%)
    pallas_call x1, Pallas kernels, tail(): pl.pallas_call(functools.partial(tail_body, chips), in_specs=[hbm] * 8 +...  202 us
    pallas_call x1, Pallas kernels, attention(): pl.pallas_call(functools.partial(attn_body, kb=kb), grid_spec=pltpu.Prefe...  128 us
    all_gather x2, blocking collectives, device_fn(): gather = lambda a: lax.all_gather(a, 'sp', axis=0, tiled=True)  38.9 us
  transfers between devices with their start and end apart: 5, of which 1 were waited for; matrix products, arithmetic and copies ran while one was open for 3% of the time, Pallas kernels for 32%

profile of v1, /device:TPU:89, one launch (start us, length us, event | category | flops | bytes accessed | tf_op | source)
XLA Modules:
  0.0 402.4 jit_solution(11982137576684111493)
XLA Ops:
  6.6 3.9 multiply_reduce_fusion
  10.5 0.9 multiply_convert_fusion
  11.5 3.1 fusion.11
  14.6 0.1 multiply_reduce_fusion.1
  14.7 0.8 multiply_convert_fusion.1
  15.6 0.7 collective-permute-start
  16.3 0.1 collective-permute-start.1
  16.4 0.4 collective-permute-start.2
  16.8 0.6 broadcast_in_dim.2.g_ref
  17.4 24.5 %all-gather = s32[8,1,256]{2,1,0:T(1,128)S(1)} all-gather(s32[1,1,256]{2,1,0:T(1,128)S(1)} %bitcast.14), channel_id=1, replica_groups=mesh['dp'=4,'sp'=8] {'sp'}, dimensions={0}, use_global_device_ids=true | all-gather | bytes 9216 | tf_op jit(solution)/shard_map/all_gather | solution.py:422
  42.0 0.1 broadcast_multiply_fusion
  42.1 0.1 fusion.10
  42.2 0.2 fusion.9
  42.5 0.6 fusion.5
  43.0 0.1 pad_maximum_fusion.2
  43.1 14.4 %all_gather.14.kr_ref = bf16[2048,64]{1,0:T(8,128)(2,1)} all-gather(bf16[256,64]{1,0:T(8,128)(2,1)S(1)} %pad_maximum_fusion.2), channel_id=1, replica_groups=mesh['dp'=4,'sp'=8] {'sp'}, dimensions={0}, use_global_device_ids=true | all-gather | bytes 294912 | tf_op jit(solution)/shard_map/all_gather | solution.py:422
  57.6 1.0 fusion.8
  58.6 1.3 pad_maximum_fusion
  59.8 0.5 minimum_maximum_fusion
  60.4 2.1 constant_dynamic-slice_fusion
  62.4 0.5 all-gather.4.cloned.1.call-done.ckv_ref
  63.0 128.1 %shard_map.127.o_hbm = bf16[512,8192]{1,0:T(8,128)(2,1)} custom-call(s32[1]{0:T(128)} %bitcast.core_ref, s32[2]{0:T(128)} %get-tuple-element.8.lo_ref, s32[2]{0:T(128)} %get-tuple-element.7.mid_ref, s32[2]{0:T(128)} %copy-done.4, bf16[2048,512]{1,0:T(8,128)(2,1)} %all-gather.4.cloned.1.call-done.ckv_ref, bf16[2048,64]{1,0:T(8,128)(2,1)} %all_gather.14.kr_ref, ...), custom_call_target="tpu_custom_call" | custom-call | flops 80000000000 | bytes 45000000 | tf_op jit(solution)/shard_map/pallas_call | solution.py:115
  191.1 202.0 %shard_map.128 = bf16[256,2560]{1,0:T(8,128)(2,1)} custom-call(bf16[512,8192]{1,0:T(8,128)(2,1)} %shard_map.127.o_hbm, bf16[16384,2560]{1,0:T(8,128)(2,1)} %wo_hbm.1, bf16[2560,768]{1,0:T(8,128)(2,1)} %wg_hbm.1, bf16[2560,768]{1,0:T(8,128)(2,1)} %collective-permute-done.wg2_hbm, bf16[2560,768]{1,0:T(8,128)(2,1)} %wu_hbm.1, ...), custom_call_target="tpu_custom_call" | custom-call | flops 46000001024 | bytes 75000000 | tf_op jit(solution)/shard_map/pallas_call | solution.py:368
  393.1 2.5 copy.30
  (30 shorter events, 0.3 us)
Async XLA Ops:
  6.5 5.0 %copy-start.6 = (bf16[256,2560]{1,0:T(8,128)(2,1)S(1)}, bf16[256,2560]{1,0:T(8,128)(2,1)}, u32[]{:S(2)}) copy-start(bf16[256,2560]{1,0:T(8,128)(2,1)} %param.14) | copy-start | bytes 3932164
  6.5 3.9 copy-start.3
  6.6 4.9 %copy-start.5 = (bf16[512]{0:T(512)(128)(2,1)S(1)}, bf16[512]{0:T(512)(128)(2,1)}, u32[]{:S(2)}) copy-start(bf16[512]{0:T(512)(128)(2,1)} %param.20) | copy-start | bytes 3076
  6.6 53.8 %all-gather.6.cloned.1.call-start = ((), (), s32[]{:S(2)}) async-start(), calls=%async_computation.1 | async-start | bytes 3538944 | tf_op jit(solution)/shard_map/all_gather | solution.py:422
  11.4 51.6 %all-gather.4.cloned.1.call-start = ((), (), s32[]{:S(2)}) async-start(), calls=%async_computation | async-start | bytes 2359296 | tf_op jit(solution)/shard_map/all_gather | solution.py:422
  11.5 5.3 %copy-start.2 = (s32[256]{0:T(256)S(1)}, s32[256]{0:T(256)}, u32[]{:S(2)}) copy-start(s32[256]{0:T(256)} %param.15) | copy-start | bytes 3076
  11.5 5.3 %copy-start.1 = (bf16[2560]{0:T(1024)(128)(2,1)S(1)}, bf16[2560]{0:T(1024)(128)(2,1)}, u32[]{:S(2)}) copy-start(bf16[2560]{0:T(1024)(128)(2,1)} %param.23) | copy-start | bytes 15364
  15.6 175.5 %collective-permute-start = (bf16[2560,768]{1,0:T(8,128)(2,1)}, bf16[2560,768]{1,0:T(8,128)(2,1)}, u32[]{:S(2)}, u32[]{:S(2)}) collective-permute-start(bf16[2560,768]{1,0:T(8,128)(2,1)} %wg_hbm.1), channel_id=1, source_target_pairs={{0,1},{1,0},{2,3},{3,2},{4,5},{5,4},{6,7},{7,6},{8,9},{9,8},{10,11... | collective-permute-start | bytes 11796488 | tf_op jit(solution)/shard_map/ppermute | solution.py:410
  16.3 174.8 %collective-permute-start.1 = (bf16[2560,768]{1,0:T(8,128)(2,1)}, bf16[2560,768]{1,0:T(8,128)(2,1)}, u32[]{:S(2)}, u32[]{:S(2)}) collective-permute-start(bf16[2560,768]{1,0:T(8,128)(2,1)} %wu_hbm.1), channel_id=1, source_target_pairs={{0,1},{1,0},{2,3},{3,2},{4,5},{5,4},{6,7},{7,6},{8,9},{9,8},{10,11... | collective-permute-start | bytes 11796488 | tf_op jit(solution)/shard_map/ppermute | solution.py:411
  16.4 174.7 %collective-permute-start.2 = (bf16[768,2560]{1,0:T(8,128)(2,1)}, bf16[768,2560]{1,0:T(8,128)(2,1)}, u32[]{:S(2)}, u32[]{:S(2)}) collective-permute-start(bf16[768,2560]{1,0:T(8,128)(2,1)} %wd_hbm.1), channel_id=1, source_target_pairs={{0,1},{1,0},{2,3},{3,2},{4,5},{5,4},{6,7},{7,6},{8,9},{9,8},{10,11... | collective-permute-start | bytes 11796488 | tf_op jit(solution)/shard_map/ppermute | solution.py:412
  42.1 20.9 %copy-start.4 = (s32[2]{0:T(128)}, s32[2]{0:T(128)S(1)}, u32[]{:S(2)}) copy-start(s32[2]{0:T(128)S(1)} %get-tuple-element.10.blk_ref) | copy-start | bytes 28
  42.2 20.8 %copy-start = (s32[2,1,256]{2,1,0:T(1,128)}, s32[2,1,256]{2,1,0:T(1,128)S(1)}, u32[]{:S(2)}) copy-start(s32[2,1,256]{2,1,0:T(1,128)S(1)} %add_subtract_fusion.start_ref) | copy-start | bytes 6148
Sparse Core Ops, SparseCore 0:
  11.5 27.4 all-gather.5
  40.7 22.2 all-gather.3

commit v2 on v1

--- a/solution.py
+++ b/solution.py
@@ -31,23 +31,152 @@
     return jnp.cos(angles), jnp.sin(angles)
 
 
-def attn_body(core_ref, lo_ref, mid_ref, blk_ref, ckv_ref, kr_ref, cqa_ref, cqb_ref, cos_ref, sin_ref, start_ref,
+def latent_body(chips, x_ref, wdq_ref, gq_ref, wdkv_ref, gkv_ref, tab_ref,
+                kvr_ref, cqa_ref, cqb_ref, taba_ref, tabb_ref, cq_s,
+                rs_sem, rr_sem, fs_sem, fr_sem, ps_sem, pr_sem, qs_sem, qr_sem):
+    me = lax.axis_index('sp')
+    chip, core = me // 2, me % 2
+    right, left = (chip + 1) % chips, (chip + chips - 1) % chips
+    far = (chip + 2) % chips
+    ring = (2 * right + core, 2 * left + core)
+    src = (left, right)
+    peer = 2 * chip + 1 - core
+    mirror = chips - 1 - chip
+    blk = x_ref.shape[0]
+    half = blk // 2
+
+    def remote(s, d, ssem, rsem, dev):
+        return pltpu.make_async_remote_copy(src_ref=s, dst_ref=d, send_sem=ssem, recv_sem=rsem,
+                                            device_id={'sp': dev}, device_id_type=pl.DeviceIdType.MESH)
+
+    barrier = pltpu.get_barrier_semaphore()
+    for dev in (peer,) + ring + (2 * mirror + 1 - core,):
+        pl.semaphore_signal(barrier, inc=1, device_id={'sp': dev}, device_id_type=pl.DeviceIdType.MESH)
+
+    def block(c, k, part=None):
+        start = (2 * c + k) * blk
+        if part is None:
+            return kvr_ref.at[pl.ds(pl.multiple_of(start, blk), blk), :]
+        return kvr_ref.at[pl.ds(pl.multiple_of(start + part * half, half), half), :]
+
+    def ring_copy(d, c):
+        return remote(block(c, core), block(c, core), rs_sem.at[d], rr_sem.at[d], ring[d])
+
+    def fwd_copy(d, c):
+        return remote(block(c, core, d), block(c, core, d), fs_sem.at[d], fr_sem.at[d], ring[d])
+
+    def peer_copy(i, c, k, part=None):
+        return remote(block(c, k, part), block(c, k, part), ps_sem.at[i], pr_sem.at[i], peer)
+
+    x = x_ref[...]
+    lat = wdkv_ref.shape[1] - ROPE_DIM
+    kv = jnp.dot(x, wdkv_ref[:, :lat], preferred_element_type=F32)
+    c_kv = rms_norm(kv, gkv_ref[...]).astype(BF16)
+    kr = jnp.dot(x, wdkv_ref[:, lat:], preferred_element_type=F32)
+    hd = ROPE_DIM // 2
+    cosine, sine = tab_ref[:, :hd], tab_ref[:, hd:2 * hd]
+    lo_half, hi_half = kr[:, :hd], kr[:, hd:]
+    kr = jnp.concatenate([lo_half * cosine - hi_half * sine, hi_half * cosine + lo_half * sine,
+                          jnp.zeros((blk, ROPE_DIM), F32)], axis=1)
+    own = pl.ds(pl.multiple_of(me * blk, blk), blk)
+    kvr_ref[own, :lat] = c_kv
+    kvr_ref[own, lat:] = kr.astype(BF16)
+
+    pl.semaphore_wait(barrier, 4)
+    for d in range(2):
+        ring_copy(d, chip).start()
+    peer_copy(0, chip, core).start()
+
+    cq_s[...] = rms_norm(jnp.dot(x, wdq_ref[...], preferred_element_type=F32), gq_ref[...]).astype(BF16)
+    pairs = ((0, cq_s, cqa_ref, cqb_ref), (1, tab_ref, taba_ref, tabb_ref))
+
+    def qa_copy(i, s, a):
+        return remote(s, a, qs_sem.at[i], qr_sem.at[i], peer)
+
+    def qb_copy(i, s, b, k):
+        return remote(s, b, qs_sem.at[2 * k + i], qr_sem.at[2 + i], 2 * mirror + k)
+
+    @pl.when(core == 0)
+    def _():
+        for i, s, a, b in pairs:
+            qa_copy(i, s, a).start()
+        cqa_ref[...] = cq_s[...]
+        taba_ref[...] = tab_ref[...]
+
+    @pl.when(core == 1)
+    def _():
+        for i, s, a, b in pairs:
+            for k in range(2):
+                qb_copy(i, s, b, k).start()
+
+    for d in range(2):
+        ring_copy(d, src[d]).wait_recv()
+        fwd_copy(d, src[d]).start()
+        peer_copy(1 + d, src[d], core).start()
+    for d in range(2):
+        fwd_copy(d, far).wait_recv()
+        peer_copy(3 + d, far, core, d).start()
+
+    for i, s, a, b in pairs:
+        qb_copy(i, s, b, 0).wait_recv()
+
+    @pl.when(core == 1)
+    def _():
+        for i, s, a, b in pairs:
+            qa_copy(i, s, a).wait_recv()
+            for k in range(2):
+                qb_copy(i, s, b, k).wait_send()
+
+    @pl.when(core == 0)
+    def _():
+        for i, s, a, b in pairs:
+            qa_copy(i, s, a).wait_send()
+
+    other = 1 - core
+    waits = ((0, chip, None), (1, left, None), (2, right, None), (3, far, 0), (4, far, 1))
+    for i, c, part in waits:
+        peer_copy(i, c, other, part).wait_recv()
+    for i, c, part in waits:
+        peer_copy(i, c, core, part).wait_send()
+    for d in range(2):
+        ring_copy(d, chip).wait_send()
+        fwd_copy(d, src[d]).wait_send()
+
+
+def latents(chips, x, w_dq, g_q, w_dkv, g_kv, tab):
+    blk = x.shape[0]
+    lat = w_dkv.shape[1] - ROPE_DIM
+    tok = 2 * chips * blk
+    dma = pltpu.SemaphoreType.DMA
+    vmem = pl.BlockSpec(memory_space=pltpu.VMEM)
+    shape = jax.ShapeDtypeStruct
+    return pl.pallas_call(
+        functools.partial(latent_body, chips),
+        in_specs=[vmem] * 6,
+        out_specs=[vmem] * 5,
+        out_shape=[shape((tok, lat + 2 * ROPE_DIM), BF16), shape((blk, w_dq.shape[1]), BF16),
+                   shape((blk, w_dq.shape[1]), BF16), shape(tab.shape, F32), shape(tab.shape, F32)],
+        scratch_shapes=[pltpu.VMEM((blk, w_dq.shape[1]), BF16)] + [dma((2,))] * 4 + [dma((5,))] * 2 + [dma((4,))] * 2,
+        compiler_params=pltpu.CompilerParams(collective_id=1, has_side_effects=True, vmem_limit_bytes=40 * 2 ** 20),
+        cost_estimate=pl.CostEstimate(flops=2 * 10 ** 9, bytes_accessed=10 ** 7, transcendentals=0),
+    )(x, w_dq, g_q[None, :], w_dkv, g_kv[None, :], tab)
+
+
+def attn_body(core_ref, lo_ref, mid_ref, blk_ref, kvr_ref, cqa_ref, cqb_ref, cos_ref, sin_ref, start_ref,
               wuq_ref, wukv_ref, o_ref, kcat, vt, qcat, sbuf, mbuf, acc, *, kb):
     i = pl.program_id(0)
-    tok = ckv_ref.shape[0]
+    tok = kvr_ref.shape[0]
     qb = cqa_ref.shape[0]
     cur, prev = i % 2, (i + 1) % 2
 
     @pl.when(i == 0)
     def _():
-        kr = kr_ref[...]
-        pad = jnp.concatenate([kr, jnp.zeros_like(kr)], axis=1)
         for h in range(2):
-            kcat[h, :, NOPE_DIM:] = pad
+            kcat[h, :, NOPE_DIM:] = kvr_ref[:, KV_LATENT:]
 
     for r in range(tok // 512):
         rows = pl.ds(r * 512, 512)
-        e = jnp.dot(ckv_ref[rows, :], wukv_ref[...], preferred_element_type=F32).astype(BF16)
+        e = jnp.dot(kvr_ref[rows, :KV_LATENT], wukv_ref[...], preferred_element_type=F32).astype(BF16)
         for h in range(2):
             kcat[h, rows, :NOPE_DIM] = e[:, KV_DIM * h:KV_DIM * h + NOPE_DIM]
             vt[cur, h, :, rows] = e[:, KV_DIM * h + NOPE_DIM:KV_DIM * (h + 1)].T
@@ -105,8 +234,8 @@
     lax.fori_loop(0, 2, q_block, 0)
 
 
-def attention(core, lo, mid, blk, ckv, kr, cqa, cqb, cos, sin, start, w_uq, w_ukv, kb):
-    tok = ckv.shape[0]
+def attention(core, lo, mid, blk, kvr, cqa, cqb, cos, sin, start, w_uq, w_ukv, kb):
+    tok = kvr.shape[0]
     qb, q_lat = cqa.shape
     heads = w_uq.shape[1] // QK_DIM
     pairs = heads // 4
@@ -118,7 +247,7 @@
             num_scalar_prefetch=4,
             grid=(pairs + 1,),
             in_specs=[
-                full(ckv.shape), full(kr.shape), full(cqa.shape), full(cqb.shape), full(cos.shape), full(sin.shape),
+                full(kvr.shape), full(cqa.shape), full(cqb.shape), full(cos.shape), full(sin.shape),
                 full(start.shape),
                 pl.BlockSpec((q_lat, 2 * QK_DIM), lambda i, core, *_: (0, group(i, core))),
                 pl.BlockSpec((KV_LATENT, 2 * KV_DIM), lambda i, core, *_: (0, group(i, core))),
@@ -135,7 +264,7 @@
         out_shape=jax.ShapeDtypeStruct((2 * qb, heads // 2 * VALUE_DIM), BF16),
         compiler_params=pltpu.CompilerParams(dimension_semantics=("arbitrary",), vmem_limit_bytes=62 * 2 ** 20),
         cost_estimate=pl.CostEstimate(flops=80 * 10 ** 9, bytes_accessed=45 * 10 ** 6, transcendentals=40 * 10 ** 6),
-    )(core, lo, mid, blk, ckv, kr, cqa, cqb, cos, sin, start, w_uq, w_ukv)
+    )(core, lo, mid, blk, kvr, cqa, cqb, cos, sin, start, w_uq, w_ukv)
 
 
 def tail_body(chips, o_hbm, wo_hbm, wg_hbm, wg2_hbm, wu_hbm, wu2_hbm, wd_hbm, wd2_hbm, g_ref, out_ref,
@@ -411,24 +540,15 @@
         w_up2 = lax.ppermute(w_up, 'sp', swap)
         w_down2 = lax.ppermute(w_down, 'sp', swap)
 
-        q_lin = jnp.dot(x_blk, w_dq, preferred_element_type=F32)
-        c_q = rms_norm(q_lin, g_q).astype(BF16)
-        kv_lin = jnp.dot(x_blk, w_dkv, preferred_element_type=F32)
-        c_kv = rms_norm(kv_lin[:, :KV_LATENT], g_kv).astype(BF16)
         cosine, sine = rope_tables(pos_blk)
-        lo_half, hi_half = kv_lin[:, KV_LATENT:KV_LATENT + ROPE_DIM // 2], kv_lin[:, KV_LATENT + ROPE_DIM // 2:]
-        k_rope = jnp.concatenate([lo_half * cosine - hi_half * sine, hi_half * cosine + lo_half * sine],
-                                 axis=-1).astype(BF16)
-        gather = lambda a: lax.all_gather(a, 'sp', axis=0, tiled=True)
-        cq_all, ckv_all, kr_all, pos_all = gather(c_q), gather(c_kv), gather(k_rope), gather(pos_blk)
+        tab = jnp.concatenate([cosine, sine, jnp.broadcast_to(pos_blk.astype(F32)[:, None], (blk_len, ROPE_DIM))], axis=1)
+        kvr, cqa, cqb, taba, tabb = latents(chips, x_blk, w_dq, g_q, w_dkv, g_kv, tab)
 
         blk = jnp.stack([2 * chip, group_size - 1 - 2 * chip]).astype(jnp.int32)
-        take = lambda a, b: lax.dynamic_slice_in_dim(a, blk[b] * blk_len, blk_len, axis=0)
-        cqa, cqb = take(cq_all, 0), take(cq_all, 1)
-        pos_q = jnp.concatenate([take(pos_all, 0), take(pos_all, 1)])
+        tab = jnp.concatenate([taba, tabb])
         rows_q = (blk[:, None] * blk_len + jnp.arange(blk_len, dtype=jnp.int32)[None, :]).reshape(-1)
-        start = rows_q - pos_q
-        cosine, sine = rope_tables(pos_q)
+        start = rows_q - tab[:, ROPE_DIM].astype(jnp.int32)
+        cosine, sine = tab[:, :ROPE_DIM // 2], tab[:, ROPE_DIM // 2:ROPE_DIM]
         cos4 = jnp.concatenate([cosine] * 4, axis=1)
         sin4 = jnp.concatenate([-sine, sine, -sine, sine], axis=1)
         kb = 2 * blk_len
@@ -437,7 +557,7 @@
         last = (blk * blk_len + blk_len - 1) // kb
         mid = jnp.maximum(jnp.minimum((start[:, 0, -1] + kb - 1) // kb, last), lo)
 
-        o = attention(core_arr, lo, mid, blk, ckv_all, kr_all, cqa, cqb, cos4, sin4, start, w_uq, w_ukv, kb)
+        o = attention(core_arr, lo, mid, blk, kvr, cqa, cqb, cos4, sin4, start, w_uq, w_ukv, kb)
         return tail(chips, o, w_o, w_gate, w_gate2, w_up, w_up2, w_down, w_down2, g_ffn[None, :])
 
     return jax.shard_map(device_fn, mesh=mesh, in_specs=(tok_spec, row_spec, row_spec, full_spec, full_spec, full_spec, full_spec, full_spec, full_spec, full_spec, full_spec, col_spec, col_spec, P('sp', None)), out_specs=tok_spec, check_vma=False)

time: 404 us -> 376 us (0.931)
  the two profiles are of different devices: /device:TPU:89 before, /device:TPU:81 now
where the time goes in v2:
time: 376 us; the launch traced here: 374 us
  Pallas kernels  355 us (94%)
  local copies, waits for them, and re-layouts  12.2 us (3%)
  other arithmetic  3.98 us (1%)
    pallas_call x1, Pallas kernels, tail(): pl.pallas_call(functools.partial(tail_body, chips), in_specs=[hbm] * 8 +...  199 us
    pallas_call x1, Pallas kernels, attention(): pl.pallas_call(functools.partial(attn_body, kb=kb), grid_spec=pltpu.Prefe...  128 us
    pallas_call x1, Pallas kernels, latents(): pl.pallas_call(functools.partial(latent_body, chips), in_specs=[vmem] * 6...  28.1 us
    unnamed x23, local copies, waits for them, and re-layouts  11.6 us
  transfers between devices with their start and end apart: 3, of which 0 were waited for; matrix products, arithmetic and copies ran while one was open for 2% of the time, Pallas kernels for 42%

profile of v2, /device:TPU:81, one launch (start us, length us, event | category | flops | bytes accessed | tf_op | source)
XLA Modules:
  0.0 374.4 jit_solution(12680585960595490321)
XLA Ops:
  0.0 2.0 collective-permute-start
  2.0 0.5 collective-permute-start.2
  2.6 0.7 convert_element_type.17
  3.2 3.4 copy.18.wdkv_ref
  6.7 0.5 multiply_cosine_fusion
  7.3 0.1 broadcast_in_dim.10
  7.4 0.1 pad_maximum_fusion.2.tab_ref
  7.5 0.0 copy-start
  7.5 2.1 copy-done
  9.6 1.3 copy-done.1
  10.9 28.1 %shard_map.127 = (bf16[2048,640]{1,0:T(8,128)(2,1)S(1)}, bf16[256,768]{1,0:T(8,128)(2,1)S(1)}, bf16[256,768]{1,0:T(8,128)(2,1)S(1)}, f32[256,128]{1,0:T(8,128)S(1)}, f32[256,128]{1,0:T(8,128)S(1)}) custom-call(bf16[256,2560]{1,0:T(8,128)(2,1)S(1)} %copy-done.1, bf16[2560,768]{1,0:T(8,128)(2,1)S(1)} %copy-done, bf16[1,768]{1,0:T(2,128)(2,1)S(1)} %broadcast_in_dim.8.gq_ref, ...), custom_call_target="tpu_custom_call" | custom-call | flops 2000000000 | bytes 10000000 | tf_op jit(solution)/shard_map/pallas_call | solution.py:153
  39.1 1.5 copy-done.2
  40.6 0.7 copy-done.3
  41.3 0.2 fusion
  41.6 0.1 slice_negate_fusion
  41.7 0.1 broadcast_multiply_fusion
  41.8 0.1 add_subtract_fusion.start_ref
  41.9 0.2 fusion.1
  42.1 0.6 broadcast_in_dim.22.g_ref
  42.7 0.6 minimum_maximum_fusion
  43.3 1.3 pad_maximum_fusion
  44.6 128.2 %shard_map.128.o_hbm = bf16[512,8192]{1,0:T(8,128)(2,1)} custom-call(s32[1]{0:T(128)} %bitcast.core_ref, s32[2]{0:T(128)} %get-tuple-element.18.lo_ref, s32[2]{0:T(128)} %get-tuple-element.17.mid_ref, s32[2]{0:T(128)} %copy-done.8, bf16[2048,640]{1,0:T(8,128)(2,1)} %copy-done.2, bf16[256,768]{1,0:T(8,128)(2,1)} %copy-done.3, bf16[256,768]{1,0:T(8,128)(2,1)} %copy-done.4, ...), custom_call_target="tpu_custom_call" | custom-call | flops 80000000000 | bytes 45000000 | tf_op jit(solution)/shard_map/pallas_call | solution.py:244
  172.8 199.2 %shard_map.129 = bf16[256,2560]{1,0:T(8,128)(2,1)} custom-call(bf16[512,8192]{1,0:T(8,128)(2,1)} %shard_map.128.o_hbm, bf16[16384,2560]{1,0:T(8,128)(2,1)} %wo_hbm.1, bf16[2560,768]{1,0:T(8,128)(2,1)} %wg_hbm.1, bf16[2560,768]{1,0:T(8,128)(2,1)} %collective-permute-done.wg2_hbm, bf16[2560,768]{1,0:T(8,128)(2,1)} %wu_hbm.1, ...), custom_call_target="tpu_custom_call" | custom-call | flops 46000001024 | bytes 75000000 | tf_op jit(solution)/shard_map/pallas_call | solution.py:497
  372.0 2.5 copy.22
  (24 shorter events, 0.1 us)
Async XLA Ops:
  0.0 6.7 %copy-start.7 = (bf16[768]{0:T(1024)(128)(2,1)S(1)}, bf16[768]{0:T(1024)(128)(2,1)}, u32[]{:S(2)}) copy-start(bf16[768]{0:T(1024)(128)(2,1)} %param.17) | copy-start | bytes 4612
  0.0 6.7 %copy-start.9 = (bf16[512]{0:T(512)(128)(2,1)S(1)}, bf16[512]{0:T(512)(128)(2,1)}, u32[]{:S(2)}) copy-start(bf16[512]{0:T(512)(128)(2,1)} %param.20) | copy-start | bytes 3076
  0.0 172.7 %collective-permute-start = (bf16[2560,768]{1,0:T(8,128)(2,1)}, bf16[2560,768]{1,0:T(8,128)(2,1)}, u32[]{:S(2)}, u32[]{:S(2)}) collective-permute-start(bf16[2560,768]{1,0:T(8,128)(2,1)} %wg_hbm.1), channel_id=1, source_target_pairs={{0,1},{1,0},{2,3},{3,2},{4,5},{5,4},{6,7},{7,6},{8,9},{9,8},{10,11... | collective-permute-start | bytes 11796488 | tf_op jit(solution)/shard_map/ppermute | solution.py:539
  2.0 170.7 %collective-permute-start.1 = (bf16[2560,768]{1,0:T(8,128)(2,1)}, bf16[2560,768]{1,0:T(8,128)(2,1)}, u32[]{:S(2)}, u32[]{:S(2)}) collective-permute-start(bf16[2560,768]{1,0:T(8,128)(2,1)} %wu_hbm.1), channel_id=1, source_target_pairs={{0,1},{1,0},{2,3},{3,2},{4,5},{5,4},{6,7},{7,6},{8,9},{9,8},{10,11... | collective-permute-start | bytes 11796488 | tf_op jit(solution)/shard_map/ppermute | solution.py:540
  2.0 170.7 %collective-permute-start.2 = (bf16[768,2560]{1,0:T(8,128)(2,1)}, bf16[768,2560]{1,0:T(8,128)(2,1)}, u32[]{:S(2)}, u32[]{:S(2)}) collective-permute-start(bf16[768,2560]{1,0:T(8,128)(2,1)} %wd_hbm.1), channel_id=1, source_target_pairs={{0,1},{1,0},{2,3},{3,2},{4,5},{5,4},{6,7},{7,6},{8,9},{9,8},{10,11... | collective-permute-start | bytes 11796488 | tf_op jit(solution)/shard_map/ppermute | solution.py:541
  7.5 2.1 copy-start
  9.6 1.3 copy-start.1
  10.9 31.2 %copy-start.6 = (bf16[2560]{0:T(1024)(128)(2,1)S(1)}, bf16[2560]{0:T(1024)(128)(2,1)}, u32[]{:S(2)}) copy-start(bf16[2560]{0:T(1024)(128)(2,1)} %param.23) | copy-start | bytes 15364
  39.1 1.5 copy-start.2
  40.6 0.7 copy-start.3
  40.6 1.0 copy-start.4
  41.8 2.8 copy-start.8
  41.9 2.7 copy-start.5

commit v3 on v2

--- a/solution.py
+++ b/solution.py
@@ -31,9 +31,9 @@
     return jnp.cos(angles), jnp.sin(angles)
 
 
-def latent_body(chips, x_ref, wdq_ref, gq_ref, wdkv_ref, gkv_ref, tab_ref,
-                kvr_ref, cqa_ref, cqb_ref, taba_ref, tabb_ref, cq_s,
-                rs_sem, rr_sem, fs_sem, fr_sem, ps_sem, pr_sem, qs_sem, qr_sem):
+def latent_body(chips, x_hbm, wdq_hbm, gq_ref, wdkv_hbm, gkv_ref, tab_ref,
+                kvr_ref, cqa_ref, cqb_ref, taba_ref, tabb_ref, cq_s, x_ref, wdq_ref, wdkv_ref,
+                in_sem, rs_sem, rr_sem, fs_sem, fr_sem, ps_sem, pr_sem, qs_sem, qr_sem):
     me = lax.axis_index('sp')
     chip, core = me // 2, me % 2
     right, left = (chip + 1) % chips, (chip + chips - 1) % chips
@@ -44,6 +44,10 @@
     mirror = chips - 1 - chip
     blk = x_ref.shape[0]
     half = blk // 2
+    loads = [pltpu.make_async_copy(s, d, in_sem.at[i])
+             for i, (s, d) in enumerate(((x_hbm, x_ref), (wdkv_hbm, wdkv_ref), (wdq_hbm, wdq_ref)))]
+    for c in loads:
+        c.start()
 
     def remote(s, d, ssem, rsem, dev):
         return pltpu.make_async_remote_copy(src_ref=s, dst_ref=d, send_sem=ssem, recv_sem=rsem,
@@ -68,11 +72,14 @@
     def peer_copy(i, c, k, part=None):
         return remote(block(c, k, part), block(c, k, part), ps_sem.at[i], pr_sem.at[i], peer)
 
+    loads[0].wait()
+    loads[1].wait()
     x = x_ref[...]
-    lat = wdkv_ref.shape[1] - ROPE_DIM
-    kv = jnp.dot(x, wdkv_ref[:, :lat], preferred_element_type=F32)
+    lat = wdkv_ref.shape[0] - ROPE_DIM
+    nt_dims = (((1,), (1,)), ((), ()))
+    kv = lax.dot_general(x, wdkv_ref[:lat, :], nt_dims, preferred_element_type=F32)
     c_kv = rms_norm(kv, gkv_ref[...]).astype(BF16)
-    kr = jnp.dot(x, wdkv_ref[:, lat:], preferred_element_type=F32)
+    kr = lax.dot_general(x, wdkv_ref[lat:, :], nt_dims, preferred_element_type=F32)
     hd = ROPE_DIM // 2
     cosine, sine = tab_ref[:, :hd], tab_ref[:, hd:2 * hd]
     lo_half, hi_half = kr[:, :hd], kr[:, hd:]
@@ -87,6 +94,7 @@
         ring_copy(d, chip).start()
     peer_copy(0, chip, core).start()
 
+    loads[2].wait()
     cq_s[...] = rms_norm(jnp.dot(x, wdq_ref[...], preferred_element_type=F32), gq_ref[...]).astype(BF16)
     pairs = ((0, cq_s, cqa_ref, cqb_ref), (1, tab_ref, taba_ref, tabb_ref))
 
@@ -145,19 +153,21 @@
 
 def latents(chips, x, w_dq, g_q, w_dkv, g_kv, tab):
     blk = x.shape[0]
-    lat = w_dkv.shape[1] - ROPE_DIM
+    lat = w_dkv.shape[0] - ROPE_DIM
     tok = 2 * chips * blk
     dma = pltpu.SemaphoreType.DMA
+    hbm = pl.BlockSpec(memory_space=pl.ANY)
     vmem = pl.BlockSpec(memory_space=pltpu.VMEM)
     shape = jax.ShapeDtypeStruct
     return pl.pallas_call(
         functools.partial(latent_body, chips),
-        in_specs=[vmem] * 6,
+        in_specs=[hbm, hbm, vmem, hbm, vmem, vmem],
         out_specs=[vmem] * 5,
         out_shape=[shape((tok, lat + 2 * ROPE_DIM), BF16), shape((blk, w_dq.shape[1]), BF16),
                    shape((blk, w_dq.shape[1]), BF16), shape(tab.shape, F32), shape(tab.shape, F32)],
-        scratch_shapes=[pltpu.VMEM((blk, w_dq.shape[1]), BF16)] + [dma((2,))] * 4 + [dma((5,))] * 2 + [dma((4,))] * 2,
-        compiler_params=pltpu.CompilerParams(collective_id=1, has_side_effects=True, vmem_limit_bytes=40 * 2 ** 20),
+        scratch_shapes=[pltpu.VMEM((blk, w_dq.shape[1]), BF16), pltpu.VMEM(x.shape, BF16),
+                        pltpu.VMEM(w_dq.shape, BF16), pltpu.VMEM(w_dkv.shape, BF16), dma((3,))] + [dma((2,))] * 4 + [dma((5,))] * 2 + [dma((4,))] * 2,
+        compiler_params=pltpu.CompilerParams(collective_id=1, has_side_effects=True, vmem_limit_bytes=62 * 2 ** 20),
         cost_estimate=pl.CostEstimate(flops=2 * 10 ** 9, bytes_accessed=10 ** 7, transcendentals=0),
     )(x, w_dq, g_q[None, :], w_dkv, g_kv[None, :], tab)
 
@@ -168,70 +178,85 @@
     tok = kvr_ref.shape[0]
     qb = cqa_ref.shape[0]
     cur, prev = i % 2, (i + 1) % 2
+    v_new, v_old = i % 3, (i + 1) % 3
+    n_piece = tok // kb
 
     @pl.when(i == 0)
     def _():
-        for h in range(2):
-            kcat[h, :, NOPE_DIM:] = kvr_ref[:, KV_LATENT:]
-
-    for r in range(tok // 512):
-        rows = pl.ds(r * 512, 512)
+        for par in range(2):
+            for h in range(2):
+                kcat[par, h, :, NOPE_DIM:] = kvr_ref[:, KV_LATENT:]
+
+    def kv_piece(pc):
+        rows = pl.ds(pl.multiple_of(pc * kb, kb), kb)
         e = jnp.dot(kvr_ref[rows, :KV_LATENT], wukv_ref[...], preferred_element_type=F32).astype(BF16)
         for h in range(2):
-            kcat[h, rows, :NOPE_DIM] = e[:, KV_DIM * h:KV_DIM * h + NOPE_DIM]
-            vt[cur, h, :, rows] = e[:, KV_DIM * h + NOPE_DIM:KV_DIM * (h + 1)].T
-
-    for b, cq in enumerate((cqa_ref, cqb_ref)):
-        rows = pl.ds(b * qb, qb)
-        q = jnp.dot(cq[...], wuq_ref[...], preferred_element_type=F32)
-        q_r = jnp.concatenate([q[:, NOPE_DIM:QK_DIM], q[:, QK_DIM + NOPE_DIM:]], axis=1)
-        lane = lax.broadcasted_iota(jnp.int32, q_r.shape, 1)
-        lo_half = (lane % ROPE_DIM) < (ROPE_DIM // 2)
-        swapped = jnp.where(lo_half, pltpu.roll(q_r, 2 * ROPE_DIM - ROPE_DIM // 2, 1), pltpu.roll(q_r, ROPE_DIM // 2, 1))
-        q_r = (q_r * cos_ref[rows, :] + swapped * sin_ref[rows, :]).astype(BF16)
-        zero = jnp.zeros((qb, ROPE_DIM), BF16)
-        for h in range(2):
-            qcat[b, h, :, :NOPE_DIM] = q[:, QK_DIM * h:QK_DIM * h + NOPE_DIM].astype(BF16)
-            qcat[b, h, :, NOPE_DIM:] = jnp.concatenate([q_r[:, ROPE_DIM * h:ROPE_DIM * (h + 1)], zero], axis=1)
-
-    def q_block(b, _):
-        t0 = blk_ref[b] * qb
-
-        def step(j, carry, masked):
-            k0 = pl.multiple_of(j * kb, kb)
-            krows = pl.ds(k0, kb)
-            new = []
+            kcat[cur, h, rows, :NOPE_DIM] = e[:, KV_DIM * h:KV_DIM * h + NOPE_DIM]
+            vt[v_new, h, :, rows] = e[:, KV_DIM * h + NOPE_DIM:KV_DIM * (h + 1)].T
+
+    def q_piece():
+        for b, cq in enumerate((cqa_ref, cqb_ref)):
+            rows = pl.ds(b * qb, qb)
+            q = jnp.dot(cq[...], wuq_ref[...], preferred_element_type=F32)
+            q_r = jnp.concatenate([q[:, NOPE_DIM:QK_DIM], q[:, QK_DIM + NOPE_DIM:]], axis=1)
+            lane = lax.broadcasted_iota(jnp.int32, q_r.shape, 1)
+            lo_half = (lane % ROPE_DIM) < (ROPE_DIM // 2)
+            swapped = jnp.where(lo_half, pltpu.roll(q_r, 2 * ROPE_DIM - ROPE_DIM // 2, 1),
+                                pltpu.roll(q_r, ROPE_DIM // 2, 1))
+            q_r = (q_r * cos_ref[rows, :] + swapped * sin_ref[rows, :]).astype(BF16)
+            zero = jnp.zeros((qb, ROPE_DIM), BF16)
             for h in range(2):
-                m, l = carry[2 * h], carry[2 * h + 1]
-                s = lax.dot_general(kcat[h, krows, :], qcat[b, h], (((1,), (1,)), ((), ())),
-                                    preferred_element_type=F32)
-                s = s * (SCORE_SCALE * LOG2E)
-                if masked:
-                    r = k0 + lax.broadcasted_iota(jnp.int32, s.shape, 0)
-                    t = t0 + lax.broadcasted_iota(jnp.int32, s.shape, 1)
-                    s = jnp.where((r <= t) & (r >= start_ref[b]), s, NEG)
-                m = jnp.maximum(m, jnp.max(s.reshape(kb // 8, 8, qb), axis=0))
-                p = jnp.exp2(sbuf[prev, b, h, krows, :] - mbuf[prev, b, h])
-                l = l + jnp.sum(p.reshape(kb // 8, 8, qb), axis=0)
-                acc[h] += jnp.dot(vt[prev, h, :, krows], p.astype(BF16), preferred_element_type=F32)
-                sbuf[cur, b, h, krows, :] = s
-                new += [m, l]
-            return tuple(new)
-
-        acc[...] = jnp.zeros_like(acc)
-        init = (jnp.full((8, qb), NEG, F32), jnp.zeros((8, qb), F32)) * 2
-        carry = lax.fori_loop(lo_ref[b], mid_ref[b], functools.partial(step, masked=True), init)
-        last = (t0 + qb - 1) // kb
-        carry = lax.fori_loop(mid_ref[b], last, functools.partial(step, masked=False), carry)
-        carry = step(last, carry, True)
-        for h in range(2):
-            mbuf[cur, b, h] = jnp.max(carry[2 * h], axis=0, keepdims=True)
-            l = jnp.sum(carry[2 * h + 1], axis=0, keepdims=True)
-            o = (acc[h] * (1.0 / l)).astype(BF16)
-            o_ref[pl.ds(pl.multiple_of(b * qb, qb), qb), VALUE_DIM * h:VALUE_DIM * (h + 1)] = o.T
-        return 0
-
-    lax.fori_loop(0, 2, q_block, 0)
+                qcat[cur, b, h, :, :NOPE_DIM] = q[:, QK_DIM * h:QK_DIM * h + NOPE_DIM].astype(BF16)
+                qcat[cur, b, h, :, NOPE_DIM:] = jnp.concatenate([q_r[:, ROPE_DIM * h:ROPE_DIM * (h + 1)], zero], axis=1)
+
+    @pl.when(i == 0)
+    def _():
+        q_piece()
+        lax.fori_loop(0, n_piece, lambda pc, c: (kv_piece(pc), c)[1], 0)
+
+    @pl.when(i > 0)
+    def _():
+        base = 0
+        for b in range(2):
+            t0 = blk_ref[b] * qb
+            lo = lo_ref[b]
+            last = (t0 + qb - 1) // kb
+
+            def step(j, carry, masked, piece, b=b, t0=t0):
+                k0 = pl.multiple_of(j * kb, kb)
+                krows = pl.ds(k0, kb)
+                new = []
+                for h in range(2):
+                    m, l = carry[2 * h], carry[2 * h + 1]
+                    p = jnp.exp2(sbuf[b, h, krows, :] - mbuf[b, h])
+                    s = lax.dot_general(kcat[prev, h, krows, :], qcat[prev, b, h], (((1,), (1,)), ((), ())),
+                                        preferred_element_type=F32)
+                    s = s * (SCORE_SCALE * LOG2E)
+                    if masked:
+                        r = k0 + lax.broadcasted_iota(jnp.int32, s.shape, 0)
+                        t = t0 + lax.broadcasted_iota(jnp.int32, s.shape, 1)
+                        s = jnp.where((r <= t) & (r >= start_ref[b]), s, NEG)
+                    m = jnp.maximum(m, jnp.max(s.reshape(kb // 8, 8, qb), axis=0))
+                    l = l + jnp.sum(p.reshape(kb // 8, 8, qb), axis=0)
+                    acc[h] += jnp.dot(vt[v_old, h, :, krows], p.astype(BF16), preferred_element_type=F32)
+                    sbuf[b, h, krows, :] = s
+                    new += [m, l]
+                piece(j)
+                return tuple(new)
+
+            piece = lambda j, off=base - lo: kv_piece(off + j)
+            acc[...] = jnp.zeros_like(acc)
+            carry = (jnp.full((8, qb), NEG, F32), jnp.zeros((8, qb), F32)) * 2
+            carry = lax.fori_loop(lo, mid_ref[b], functools.partial(step, masked=True, piece=piece), carry)
+            carry = lax.fori_loop(mid_ref[b], last, functools.partial(step, masked=False, piece=piece), carry)
+            carry = step(last, carry, True, piece if b == 0 else lambda j: q_piece())
+            base = base + (last - lo + 1 if b == 0 else last - lo)
+            for h in range(2):
+                mbuf[b, h] = jnp.max(carry[2 * h], axis=0, keepdims=True)
+                l = jnp.sum(carry[2 * h + 1], axis=0, keepdims=True)
+                o = (acc[h] * (1.0 / l)).astype(BF16)
+                o_ref[pl.ds(b * qb, qb), VALUE_DIM * h:VALUE_DIM * (h + 1)] = o.T
+        lax.fori_loop(base, n_piece, lambda pc, c: (kv_piece(pc), c)[1], 0)
 
 
 def attention(core, lo, mid, blk, kvr, cqa, cqb, cos, sin, start, w_uq, w_ukv, kb):
@@ -245,20 +270,19 @@
         functools.partial(attn_body, kb=kb),
         grid_spec=pltpu.PrefetchScalarGridSpec(
             num_scalar_prefetch=4,
-            grid=(pairs + 1,),
+            grid=(pairs + 2,),
             in_specs=[
-                full(kvr.shape), full(cqa.shape), full(cqb.shape), full(cos.shape), full(sin.shape),
-                full(start.shape),
+                full(kvr.shape), full(cqa.shape), full(cqb.shape), full(cos.shape), full(sin.shape), full(start.shape),
                 pl.BlockSpec((q_lat, 2 * QK_DIM), lambda i, core, *_: (0, group(i, core))),
                 pl.BlockSpec((KV_LATENT, 2 * KV_DIM), lambda i, core, *_: (0, group(i, core))),
             ],
-            out_specs=pl.BlockSpec((2 * qb, 2 * VALUE_DIM), lambda i, *_: (0, jnp.maximum(i - 1, 0))),
+            out_specs=pl.BlockSpec((2 * qb, 2 * VALUE_DIM), lambda i, *_: (0, jnp.maximum(i - 2, 0))),
             scratch_shapes=[
-                pltpu.VMEM((2, tok, 2 * NOPE_DIM), BF16),
-                pltpu.VMEM((2, 2, VALUE_DIM, tok), BF16),
-                pltpu.VMEM((2, 2, qb, 2 * NOPE_DIM), BF16),
-                pltpu.VMEM((2, 2, 2, tok, qb), F32),
-                pltpu.VMEM((2, 2, 2, 1, qb), F32),
+                pltpu.VMEM((2, 2, tok, 2 * NOPE_DIM), BF16),
+                pltpu.VMEM((3, 2, VALUE_DIM, tok), BF16),
+                pltpu.VMEM((2, 2, 2, qb, 2 * NOPE_DIM), BF16),
+                pltpu.VMEM((2, 2, tok, qb), F32),
+                pltpu.VMEM((2, 2, 1, qb), F32),
                 pltpu.VMEM((2, VALUE_DIM, qb), F32),
             ]),
         out_shape=jax.ShapeDtypeStruct((2 * qb, heads // 2 * VALUE_DIM), BF16),
@@ -536,13 +560,13 @@
         blk_len = x_blk.shape[0]
         core_arr = core.reshape(1).astype(jnp.int32)
 
-        w_gate2 = lax.ppermute(w_gate, 'sp', swap)
-        w_up2 = lax.ppermute(w_up, 'sp', swap)
-        w_down2 = lax.ppermute(w_down, 'sp', swap)
-
         cosine, sine = rope_tables(pos_blk)
         tab = jnp.concatenate([cosine, sine, jnp.broadcast_to(pos_blk.astype(F32)[:, None], (blk_len, ROPE_DIM))], axis=1)
-        kvr, cqa, cqb, taba, tabb = latents(chips, x_blk, w_dq, g_q, w_dkv, g_kv, tab)
+        kvr, cqa, cqb, taba, tabb = latents(chips, x_blk, w_dq, g_q, w_dkv.T, g_kv, tab)
+        kvr, late_gate, late_up, late_down = lax.optimization_barrier((kvr, w_gate, w_up, w_down))
+        w_gate2 = lax.ppermute(late_gate, 'sp', swap)
+        w_up2 = lax.ppermute(late_up, 'sp', swap)
+        w_down2 = lax.ppermute(late_down, 'sp', swap)
 
         blk = jnp.stack([2 * chip, group_size - 1 - 2 * chip]).astype(jnp.int32)
         tab = jnp.concatenate([taba, tabb])

time: 376 us -> 363 us (0.965)
  Pallas kernels: 355 us -> 350 us
  local copies, waits for them, and re-layouts: 12.2 us -> 7.5 us
    pallas_call x1, Pallas kernels: 199 us -> 180 us  [tail(): pl.pallas_call(functools.partial(tail_body, chips), in_specs=[hbm] * 8 +...]
    unnamed x23 -> x8, local copies, waits for them, and re-layouts: 11.6 us -> 3.38 us
    pallas_call x1, Pallas kernels: 128 us -> 135 us  [attention(): pl.pallas_call(functools.partial(attn_body, kb=kb), grid_spec=pltpu.Prefe...]
    pallas_call x1, Pallas kernels: 28.1 us -> 34.6 us  [latents(): pl.pallas_call(functools.partial(latent_body, chips), in_specs=[hbm, hbm,...]
  transfers between devices with their start and end apart: 3 -> 3, of which waited for: 0 -> 0; matrix products, arithmetic and copies ran while one was open for 2% -> 1% of each run, Pallas kernels for 42% -> 37%
where the time goes in v3:
time: 363 us
  Pallas kernels  350 us (96%)
  local copies, waits for them, and re-layouts  7.5 us (2%)
  other arithmetic  4.57 us (1%)
    pallas_call x1, Pallas kernels, tail(): pl.pallas_call(functools.partial(tail_body, chips), in_specs=[hbm] * 8 +...  180 us
    pallas_call x1, Pallas kernels, attention(): pl.pallas_call(functools.partial(attn_body, kb=kb), grid_spec=pltpu.Prefe...  135 us
    pallas_call x1, Pallas kernels, latents(): pl.pallas_call(functools.partial(latent_body, chips), in_specs=[hbm, hbm,...  34.6 us
  transfers between devices with their start and end apart: 3, of which 0 were waited for; matrix products, arithmetic and copies ran while one was open for 1% of the time, Pallas kernels for 37%

profile of v3, /device:TPU:81, one launch (start us, length us, event | category | flops | bytes accessed | tf_op | source)
XLA Modules:
  0.0 362.7 jit_solution(1293140493922544463)
XLA Ops:
  0.0 0.7 convert_element_type.17
  0.7 1.3 broadcast_in_dim.8.gq_ref
  2.0 1.2 broadcast_in_dim.9.gkv_ref
  3.2 0.5 multiply_cosine_fusion
  3.7 0.1 broadcast_in_dim.10
  3.8 0.8 pad_maximum_fusion.2.tab_ref
  4.6 34.6 %shard_map.127 = (bf16[2048,640]{1,0:T(8,128)(2,1)}, bf16[256,768]{1,0:T(8,128)(2,1)}, bf16[256,768]{1,0:T(8,128)(2,1)}, f32[256,128]{1,0:T(8,128)}, f32[256,128]{1,0:T(8,128)}) custom-call(bf16[256,2560]{1,0:T(8,128)(2,1)} %x_hbm.1, bf16[2560,768]{1,0:T(8,128)(2,1)} %wdq_hbm.1, bf16[1,768]{1,0:T(2,128)(2,1)} %broadcast_in_dim.8.gq_ref, ...), custom_call_target="tpu_custom_call" | custom-call | flops 2000000000 | bytes 10000000 | tf_op jit(solution)/shard_map/pallas_call | solution.py:162
  39.3 0.5 collective-permute-start
  39.8 0.1 collective-permute-start.1
  39.9 0.4 collective-permute-start.2
  40.3 0.9 constant_dynamic-update-slice_fusion.1
  41.2 0.9 constant_dynamic-update-slice_fusion
  42.1 0.2 fusion
  42.3 0.1 slice_negate_fusion
  42.5 0.1 broadcast_multiply_fusion
  42.6 0.1 add_subtract_fusion.start_ref
  42.6 0.2 fusion.1
  42.9 0.6 broadcast_in_dim.22.g_ref
  43.5 0.5 minimum_maximum_fusion
  44.0 1.3 pad_maximum_fusion
  45.3 135.0 %shard_map.128.o_hbm = bf16[512,8192]{1,0:T(8,128)(2,1)} custom-call(s32[1]{0:T(128)} %bitcast.core_ref, s32[2]{0:T(128)} %get-tuple-element.26.lo_ref, s32[2]{0:T(128)} %get-tuple-element.25.mid_ref, s32[2]{0:T(128)} %copy-done.2, bf16[2048,640]{1,0:T(8,128)(2,1)} %get-tuple-element.17.kvr_ref, bf16[256,768]{1,0:T(8,128)(2,1)} %get-tuple-element.18.cqa_ref, ...), custom_call_target="tpu_custom_call" | custom-call | flops 80000000000 | bytes 45000000 | tf_op jit(solution)/shard_map/pallas_call | solution.py:269
  180.3 0.0 collective-permute-done.wg2_hbm
  180.3 179.9 %shard_map.129 = bf16[256,2560]{1,0:T(8,128)(2,1)} custom-call(bf16[512,8192]{1,0:T(8,128)(2,1)} %shard_map.128.o_hbm, bf16[16384,2560]{1,0:T(8,128)(2,1)} %wo_hbm.1, bf16[2560,768]{1,0:T(8,128)(2,1)} %wg_hbm.1, bf16[2560,768]{1,0:T(8,128)(2,1)} %collective-permute-done.wg2_hbm, bf16[2560,768]{1,0:T(8,128)(2,1)} %wu_hbm.1, ...), custom_call_target="tpu_custom_call" | custom-call | flops 46000001024 | bytes 75000000 | tf_op jit(solution)/shard_map/pallas_call | solution.py:521
  360.2 2.5 copy.19
  (9 shorter events, 0.0 us)
Async XLA Ops:
  4.6 38.2 %copy-start.1 = (bf16[2560]{0:T(1024)(128)(2,1)S(1)}, bf16[2560]{0:T(1024)(128)(2,1)}, u32[]{:S(2)}) copy-start(bf16[2560]{0:T(1024)(128)(2,1)} %param.23) | copy-start | bytes 15364
  39.3 141.0 %collective-permute-start = (bf16[2560,768]{1,0:T(8,128)(2,1)}, bf16[2560,768]{1,0:T(8,128)(2,1)}, u32[]{:S(2)}, u32[]{:S(2)}) collective-permute-start(bf16[2560,768]{1,0:T(8,128)(2,1)} %wg_hbm.1), channel_id=1, source_target_pairs={{0,1},{1,0},{2,3},{3,2},{4,5},{5,4},{6,7},{7,6},{8,9},{9,8},{10,11... | collective-permute-start | bytes 11796488 | tf_op jit(solution)/shard_map/ppermute | solution.py:567
  39.8 140.5 %collective-permute-start.1 = (bf16[2560,768]{1,0:T(8,128)(2,1)}, bf16[2560,768]{1,0:T(8,128)(2,1)}, u32[]{:S(2)}, u32[]{:S(2)}) collective-permute-start(bf16[2560,768]{1,0:T(8,128)(2,1)} %wu_hbm.1), channel_id=1, source_target_pairs={{0,1},{1,0},{2,3},{3,2},{4,5},{5,4},{6,7},{7,6},{8,9},{9,8},{10,11... | collective-permute-start | bytes 11796488 | tf_op jit(solution)/shard_map/ppermute | solution.py:568
  39.9 140.4 %collective-permute-start.2 = (bf16[768,2560]{1,0:T(8,128)(2,1)}, bf16[768,2560]{1,0:T(8,128)(2,1)}, u32[]{:S(2)}, u32[]{:S(2)}) collective-permute-start(bf16[768,2560]{1,0:T(8,128)(2,1)} %wd_hbm.1), channel_id=1, source_target_pairs={{0,1},{1,0},{2,3},{3,2},{4,5},{5,4},{6,7},{7,6},{8,9},{9,8},{10,11... | collective-permute-start | bytes 11796488 | tf_op jit(solution)/shard_map/ppermute | solution.py:569
  42.6 2.7 copy-start.2
  42.6 2.6 copy-start

commit v4 on v3

--- a/solution.py
+++ b/solution.py
@@ -54,7 +54,7 @@
                                             device_id={'sp': dev}, device_id_type=pl.DeviceIdType.MESH)
 
     barrier = pltpu.get_barrier_semaphore()
-    for dev in (peer,) + ring + (2 * mirror + 1 - core,):
+    for dev in (peer,) + ring:
         pl.semaphore_signal(barrier, inc=1, device_id={'sp': dev}, device_id_type=pl.DeviceIdType.MESH)
 
     def block(c, k, part=None):
@@ -89,7 +89,7 @@
     kvr_ref[own, :lat] = c_kv
     kvr_ref[own, lat:] = kr.astype(BF16)
 
-    pl.semaphore_wait(barrier, 4)
+    pl.semaphore_wait(barrier, 3)
     for d in range(2):
         ring_copy(d, chip).start()
     peer_copy(0, chip, core).start()
@@ -101,8 +101,11 @@
     def qa_copy(i, s, a):
         return remote(s, a, qs_sem.at[i], qr_sem.at[i], peer)
 
-    def qb_copy(i, s, b, k):
-        return remote(s, b, qs_sem.at[2 * k + i], qr_sem.at[2 + i], 2 * mirror + k)
+    def qb_copy(i, s, b):
+        return remote(s, b, qs_sem.at[i], qr_sem.at[2 + i], 2 * mirror + core)
+
+    def qc_copy(i, b):
+        return remote(b, b, qs_sem.at[2 + i], qr_sem.at[2 + i], peer)
 
     @pl.when(core == 0)
     def _():
@@ -114,8 +117,7 @@
     @pl.when(core == 1)
     def _():
         for i, s, a, b in pairs:
-            for k in range(2):
-                qb_copy(i, s, b, k).start()
+            qb_copy(i, s, b).start()
 
     for d in range(2):
         ring_copy(d, src[d]).wait_recv()
@@ -125,19 +127,20 @@
         fwd_copy(d, far).wait_recv()
         peer_copy(3 + d, far, core, d).start()
 
-    for i, s, a, b in pairs:
-        qb_copy(i, s, b, 0).wait_recv()
-
     @pl.when(core == 1)
     def _():
+        for i, s, a, b in pairs:
+            qb_copy(i, s, b).wait_recv()
+            qc_copy(i, b).start()
         for i, s, a, b in pairs:
             qa_copy(i, s, a).wait_recv()
-            for k in range(2):
-                qb_copy(i, s, b, k).wait_send()
+            qb_copy(i, s, b).wait_send()
+            qc_copy(i, b).wait_send()
 
     @pl.when(core == 0)
     def _():
         for i, s, a, b in pairs:
+            qc_copy(i, b).wait_recv()
             qa_copy(i, s, a).wait_send()
 
     other = 1 - core
@@ -172,8 +175,8 @@
     )(x, w_dq, g_q[None, :], w_dkv, g_kv[None, :], tab)
 
 
-def attn_body(core_ref, lo_ref, mid_ref, blk_ref, kvr_ref, cqa_ref, cqb_ref, cos_ref, sin_ref, start_ref,
-              wuq_ref, wukv_ref, o_ref, kcat, vt, qcat, sbuf, mbuf, acc, *, kb):
+def attn_body(core_ref, lo_ref, mid_ref, blk_ref, kvr_ref, cqa_ref, cqb_ref, taba_ref, tabb_ref, start_ref,
+              wuq_ref, wukv_ref, o_ref, kcat, vt, qcat, sbuf, mbuf, acc, cos_ref, sin_ref, *, kb):
     i = pl.program_id(0)
     tok = kvr_ref.shape[0]
     qb = cqa_ref.shape[0]
@@ -186,6 +189,11 @@
         for par in range(2):
             for h in range(2):
                 kcat[par, h, :, NOPE_DIM:] = kvr_ref[:, KV_LATENT:]
+        for b, tab in enumerate((taba_ref, tabb_ref)):
+            rows = pl.ds(b * qb, qb)
+            cosine, sine = tab[:, :ROPE_DIM // 2], tab[:, ROPE_DIM // 2:ROPE_DIM]
+            cos_ref[rows, :] = jnp.concatenate([cosine] * 4, axis=1)
+            sin_ref[rows, :] = jnp.concatenate([-sine, sine, -sine, sine], axis=1)
 
     def kv_piece(pc):
         rows = pl.ds(pl.multiple_of(pc * kb, kb), kb)
@@ -259,7 +267,7 @@
         lax.fori_loop(base, n_piece, lambda pc, c: (kv_piece(pc), c)[1], 0)
 
 
-def attention(core, lo, mid, blk, kvr, cqa, cqb, cos, sin, start, w_uq, w_ukv, kb):
+def attention(core, lo, mid, blk, kvr, cqa, cqb, taba, tabb, start, w_uq, w_ukv, kb):
     tok = kvr.shape[0]
     qb, q_lat = cqa.shape
     heads = w_uq.shape[1] // QK_DIM
@@ -272,7 +280,7 @@
             num_scalar_prefetch=4,
             grid=(pairs + 2,),
             in_specs=[
-                full(kvr.shape), full(cqa.shape), full(cqb.shape), full(cos.shape), full(sin.shape), full(start.shape),
+                full(kvr.shape), full(cqa.shape), full(cqb.shape), full(taba.shape), full(tabb.shape), full(start.shape),
                 pl.BlockSpec((q_lat, 2 * QK_DIM), lambda i, core, *_: (0, group(i, core))),
                 pl.BlockSpec((KV_LATENT, 2 * KV_DIM), lambda i, core, *_: (0, group(i, core))),
             ],
@@ -284,11 +292,13 @@
                 pltpu.VMEM((2, 2, tok, qb), F32),
                 pltpu.VMEM((2, 2, 1, qb), F32),
                 pltpu.VMEM((2, VALUE_DIM, qb), F32),
+                pltpu.VMEM((2 * qb, 2 * ROPE_DIM), F32),
+                pltpu.VMEM((2 * qb, 2 * ROPE_DIM), F32),
             ]),
         out_shape=jax.ShapeDtypeStruct((2 * qb, heads // 2 * VALUE_DIM), BF16),
         compiler_params=pltpu.CompilerParams(dimension_semantics=("arbitrary",), vmem_limit_bytes=62 * 2 ** 20),
         cost_estimate=pl.CostEstimate(flops=80 * 10 ** 9, bytes_accessed=45 * 10 ** 6, transcendentals=40 * 10 ** 6),
-    )(core, lo, mid, blk, kvr, cqa, cqb, cos, sin, start, w_uq, w_ukv)
+    )(core, lo, mid, blk, kvr, cqa, cqb, taba, tabb, start, w_uq, w_ukv)
 
 
 def tail_body(chips, o_hbm, wo_hbm, wg_hbm, wg2_hbm, wu_hbm, wu2_hbm, wd_hbm, wd2_hbm, g_ref, out_ref,
@@ -398,13 +408,13 @@
         def _():
             acc[n] += prod
 
+        @pl.when((k == kt // 2) & (n >= 1))
+        def _():
+            combine(n - 1)
+
         @pl.when(k == kt - 1)
         def _():
             x_copy(n).start()
-
-            @pl.when(n >= 1)
-            def _():
-                combine(n - 1)
 
             @pl.when(n >= 3)
             def _():
@@ -442,18 +452,18 @@
     def down(slot, c, d):
         rows = pl.ds(c * half, half)
         return sum(jnp.dot(act[slot, rows, pl.ds(g * grain, grain)],
-                           obuf[pl.ds((g % per) * grain, grain), pl.ds((g // per) * width + d * hw, hw)],
+                           obuf[pl.ds((g % per) * grain, grain),
+                                pl.ds(pl.multiple_of((g // per) * width + d * hw, 256), hw)],
                            preferred_element_type=F32) for g in range(n_grain))
 
     def s_copy(d, s, c):
         src_ref = rss.at[d, c] if s == 0 else rsr.at[d, s - 1, c]
-        return remote(src_ref, rsr.at[d, s, c], ss_sem.at[d, s, c], sr_sem.at[d, s, c], ring[d])
-
-    def first():
-        for d, q in enumerate((left, right)):
-            for c in range(2):
-                rss[d, c] = down(slot_of(q), c, d)
-                s_copy(d, 0, c).start()
+        return remote(src_ref, rsr.at[d, s, c], ss_sem.at[d, s, c], sr_sem.at[d, s, c], ring[0] + d * (ring[1] - ring[0]))
+
+    def first(d):
+        for c in range(2):
+            rss[d, c] = down(slot_of(left + d * (right - left)), c, d)
+            s_copy(d, 0, c).start()
 
     for c in f_copies:
         c.wait()
@@ -463,11 +473,13 @@
     for c in d_copies:
         c.wait()
     activate(left)
+
+    @pl.when(core == 0)
+    def _():
+        first(0)
     activate(right)
-
-    @pl.when(core == 0)
-    def _():
-        first()
+    parity = chip % 2
+    first(core * parity + (1 - core))
     for n in range(nt):
         for d in range(2):
             f_copy(d, n, far).wait_recv()
@@ -475,7 +487,7 @@
 
     @pl.when(core == 1)
     def _():
-        first()
+        first(1 - parity)
 
     for s, dests in ((1, (far, far)), (2, (right, left))):
         for c in range(2):
@@ -569,19 +581,15 @@
         w_down2 = lax.ppermute(late_down, 'sp', swap)
 
         blk = jnp.stack([2 * chip, group_size - 1 - 2 * chip]).astype(jnp.int32)
-        tab = jnp.concatenate([taba, tabb])
-        rows_q = (blk[:, None] * blk_len + jnp.arange(blk_len, dtype=jnp.int32)[None, :]).reshape(-1)
-        start = rows_q - tab[:, ROPE_DIM].astype(jnp.int32)
-        cosine, sine = tab[:, :ROPE_DIM // 2], tab[:, ROPE_DIM // 2:ROPE_DIM]
-        cos4 = jnp.concatenate([cosine] * 4, axis=1)
-        sin4 = jnp.concatenate([-sine, sine, -sine, sine], axis=1)
+        pos_q = jnp.stack([taba[:, ROPE_DIM], tabb[:, ROPE_DIM]]).astype(jnp.int32)
+        start = blk[:, None] * blk_len + jnp.arange(blk_len, dtype=jnp.int32)[None, :] - pos_q
         kb = 2 * blk_len
         start = start.reshape(2, 1, blk_len)
         lo = start[:, 0, 0] // kb
         last = (blk * blk_len + blk_len - 1) // kb
         mid = jnp.maximum(jnp.minimum((start[:, 0, -1] + kb - 1) // kb, last), lo)
 
-        o = attention(core_arr, lo, mid, blk, kvr, cqa, cqb, cos4, sin4, start, w_uq, w_ukv, kb)
+        o = attention(core_arr, lo, mid, blk, kvr, cqa, cqb, taba, tabb, start, w_uq, w_ukv, kb)
         return tail(chips, o, w_o, w_gate, w_gate2, w_up, w_up2, w_down, w_down2, g_ffn[None, :])
 
     return jax.shard_map(device_fn, mesh=mesh, in_specs=(tok_spec, row_spec, row_spec, full_spec, full_spec, full_spec, full_spec, full_spec, full_spec, full_spec, full_spec, col_spec, col_spec, P('sp', None)), out_specs=tok_spec, check_vma=False)

time: 363 us -> 352 us (0.970)
  the two profiles are of different devices: /device:TPU:81 before, /device:TPU:119 now
where the time goes in v4:
time: 352 us; the launch traced here: 353 us
  Pallas kernels  342 us (97%)
  local copies, waits for them, and re-layouts  6.89 us (2%)
    pallas_call x1, Pallas kernels, tail(): pl.pallas_call(functools.partial(tail_body, chips), in_specs=[hbm] * 8 +...  167 us
    pallas_call x1, Pallas kernels, attention(): pl.pallas_call(functools.partial(attn_body, kb=kb), grid_spec=pltpu.Prefe...  149 us
    pallas_call x1, Pallas kernels, latents(): pl.pallas_call(functools.partial(latent_body, chips), in_specs=[hbm, hbm,...  25.8 us
  transfers between devices with their start and end apart: 3, of which 0 were waited for; matrix products, arithmetic and copies ran while one was open for 1% of the time, Pallas kernels for 42%

profile of v4, /device:TPU:119, one launch (start us, length us, event | category | flops | bytes accessed | tf_op | source)
XLA Modules:
  0.0 352.6 jit_solution(6568025133247284651)
XLA Ops:
  0.0 0.7 convert_element_type.14
  0.7 1.3 broadcast_in_dim.8.gq_ref
  2.0 1.2 broadcast_in_dim.9.gkv_ref
  3.2 0.5 multiply_cosine_fusion
  3.7 0.1 broadcast_in_dim.10
  3.8 0.8 pad_maximum_fusion.tab_ref
  4.6 25.8 %shard_map.127 = (bf16[2048,640]{1,0:T(8,128)(2,1)}, bf16[256,768]{1,0:T(8,128)(2,1)}, bf16[256,768]{1,0:T(8,128)(2,1)}, f32[256,128]{1,0:T(8,128)}, f32[256,128]{1,0:T(8,128)}) custom-call(bf16[256,2560]{1,0:T(8,128)(2,1)} %x_hbm.1, bf16[2560,768]{1,0:T(8,128)(2,1)} %wdq_hbm.1, bf16[1,768]{1,0:T(2,128)(2,1)} %broadcast_in_dim.8.gq_ref, ...), custom_call_target="tpu_custom_call" | custom-call | flops 2000000000 | bytes 10000000 | tf_op jit(solution)/shard_map/pallas_call | solution.py:165
  30.4 0.5 collective-permute-start
  30.9 0.1 collective-permute-start.1
  31.0 0.4 collective-permute-start.2
  31.4 0.1 broadcast_multiply_fusion
  31.5 1.2 slice_reduce_fusion
  32.7 0.1 fusion.start_ref
  32.8 0.2 fusion.1
  33.0 0.0 copy-done.1
  33.0 0.6 broadcast_in_dim.22.g_ref
  33.6 0.6 minimum_maximum_fusion
  34.2 0.0 copy-done.2
  34.2 148.6 %shard_map.128.o_hbm = bf16[512,8192]{1,0:T(8,128)(2,1)} custom-call(s32[1]{0:T(128)} %bitcast.core_ref, s32[2]{0:T(128)} %get-tuple-element.26.lo_ref, s32[2]{0:T(128)} %get-tuple-element.25.mid_ref, s32[2]{0:T(128)} %copy-done.2, bf16[2048,640]{1,0:T(8,128)(2,1)} %get-tuple-element.17.kvr_ref, bf16[256,768]{1,0:T(8,128)(2,1)} %get-tuple-element.18.cqa_ref, ...), custom_call_target="tpu_custom_call" | custom-call | flops 80000000000 | bytes 45000000 | tf_op jit(solution)/shard_map/pallas_call | solution.py:277
  182.8 0.0 collective-permute-done.wg2_hbm
  182.8 0.0 collective-permute-done.1.wu2_hbm
  182.8 0.0 collective-permute-done.2.wd2_hbm
  182.8 167.3 %shard_map.129 = bf16[256,2560]{1,0:T(8,128)(2,1)} custom-call(bf16[512,8192]{1,0:T(8,128)(2,1)} %shard_map.128.o_hbm, bf16[16384,2560]{1,0:T(8,128)(2,1)} %wo_hbm.1, bf16[2560,768]{1,0:T(8,128)(2,1)} %wg_hbm.1, bf16[2560,768]{1,0:T(8,128)(2,1)} %collective-permute-done.wg2_hbm, bf16[2560,768]{1,0:T(8,128)(2,1)} %wu_hbm.1, ...), custom_call_target="tpu_custom_call" | custom-call | flops 46000001024 | bytes 75000000 | tf_op jit(solution)/shard_map/pallas_call | solution.py:533
  350.2 2.5 copy.16
  (5 shorter events, 0.0 us)
Async XLA Ops:
  4.6 28.4 %copy-start.1 = (bf16[2560]{0:T(1024)(128)(2,1)S(1)}, bf16[2560]{0:T(1024)(128)(2,1)}, u32[]{:S(2)}) copy-start(bf16[2560]{0:T(1024)(128)(2,1)} %param.23) | copy-start | bytes 15364
  30.4 152.4 %collective-permute-start = (bf16[2560,768]{1,0:T(8,128)(2,1)}, bf16[2560,768]{1,0:T(8,128)(2,1)}, u32[]{:S(2)}, u32[]{:S(2)}) collective-permute-start(bf16[2560,768]{1,0:T(8,128)(2,1)} %wg_hbm.1), channel_id=1, source_target_pairs={{0,1},{1,0},{2,3},{3,2},{4,5},{5,4},{6,7},{7,6},{8,9},{9,8},{10,11... | collective-permute-start | bytes 11796488 | tf_op jit(solution)/shard_map/ppermute | solution.py:579
  30.9 151.9 %collective-permute-start.1 = (bf16[2560,768]{1,0:T(8,128)(2,1)}, bf16[2560,768]{1,0:T(8,128)(2,1)}, u32[]{:S(2)}, u32[]{:S(2)}) collective-permute-start(bf16[2560,768]{1,0:T(8,128)(2,1)} %wu_hbm.1), channel_id=1, source_target_pairs={{0,1},{1,0},{2,3},{3,2},{4,5},{5,4},{6,7},{7,6},{8,9},{9,8},{10,11... | collective-permute-start | bytes 11796488 | tf_op jit(solution)/shard_map/ppermute | solution.py:580
  31.0 151.8 %collective-permute-start.2 = (bf16[768,2560]{1,0:T(8,128)(2,1)}, bf16[768,2560]{1,0:T(8,128)(2,1)}, u32[]{:S(2)}, u32[]{:S(2)}) collective-permute-start(bf16[768,2560]{1,0:T(8,128)(2,1)} %wd_hbm.1), channel_id=1, source_target_pairs={{0,1},{1,0},{2,3},{3,2},{4,5},{5,4},{6,7},{7,6},{8,9},{9,8},{10,11... | collective-permute-start | bytes 11796488 | tf_op jit(solution)/shard_map/ppermute | solution.py:581
  31.5 2.7 copy-start.2
  32.8 1.4 copy-start
